TPU v7x, 256 devices: a whole 4x4x8 slice. The times are simulated.
256 devices in a mesh: cells: 32 (over z, x), genes: 8 (over y, core).
Axes of the slice: x: 4, y: 4, z: 8, core: 2. Of those that a mesh axis runs over, the one named last changes fastest.
Arguments:
- counts: int32 [155648, 4000], P('cells', 'genes'), may hold values from 0 to 674, as said below
- sketch: bfloat16 [4000, 128], P('genes'), may hold values from -6 to 6
Outputs:
- basis: float32 [155648, 128], P('cells')
- loadings: float32 [4000, 128], P('genes')
Inputs may be any that keep to these rules, and one draw needn't show every extreme that they name: `counts`: every cell and every gene has a positive total.
All inputs are finite; a program needn't handle non-finite values.
Results may differ from a plain program's by a relative error of at most 0.0051.
Values may be sent and summed in bfloat16 or wider, within the bound.
A program may use at most 128 MiB of HBM per device.

v0:
```python
import math

import jax
import jax.numpy as jnp
from jax import lax
from jax.sharding import PartitionSpec as P

ITERS = 2


def padded_to(lines, size):
    spare = -lines.shape[0] % size
    if not spare:
        return lines
    return jnp.concatenate([lines, jnp.zeros((spare, *lines.shape[1:]), lines.dtype)])


def from_everyone(array, axis):
    copies = jnp.broadcast_to(array, (lax.axis_size(axis), *array.shape))
    return lax.all_to_all(copies, axis, split_axis=0, concat_axis=0, tiled=True)


def laid_out(parts, dim):
    shape = list(parts.shape[1:])
    shape[dim] *= parts.shape[0]
    return jnp.moveaxis(parts, 0, dim).reshape(shape)


def gathered_copies(array, axis, dim):
    parts = from_everyone(array, axis)
    return laid_out(parts, dim)


def split_up(array, dim, size):
    before, after = (array.shape[:dim], array.shape[dim + 1 :])
    return jnp.moveaxis(array.reshape(*before, size, -1, *after), dim, 0)


def summed_on_arrival(array, axis, dim):
    size = lax.axis_size(axis)
    parts = lax.all_to_all(split_up(array, dim, size), axis, 0, 0, tiled=True)
    return jnp.sum(parts, axis=0)


def total_of(array, axes):
    lines = array.reshape(-1)
    padded = padded_to(lines, lax.axis_size(axes))
    whole = gathered_copies(summed_on_arrival(padded, axes, 0), axes, 0)
    return lax.slice_in_dim(whole, 0, len(lines)).reshape(array.shape)


def of_everyone(array, axis):
    return from_everyone(array, axis).sum(axis=0)


def in_one(arrays, axis):
    ends = [0]
    for a in arrays:
        ends.append(ends[-1] + a.size)
    subtotal = of_everyone(jnp.concatenate([a.ravel() for a in arrays]), axis)
    return tuple((subtotal[b:e].reshape(a.shape) for a, b, e in zip(arrays, ends, ends[1:])))


def total_of_2(array, axes):
    lines = array.reshape(-1, array.shape[-1])
    own = summed_on_arrival(padded_to(lines, lax.axis_size(axes)), axes, 0)
    whole = gathered_copies(own, axes, 0)
    return whole[: len(lines)].reshape(array.shape)


def residual_block(block, cell_total, frac, limit):
    values = block.astype(jnp.float32)
    expected = cell_total[:, None] * frac[None, :]
    scaled = (values - expected) / jnp.sqrt(expected + 0.01 * expected * expected)
    return jnp.clip(scaled, -limit, limit).astype(jnp.bfloat16)


def self_gram(block):
    return lax.dot_general(
        block,
        block,
        (((0,), (0,)), ((), ())),
        precision=lax.Precision.HIGHEST,
        preferred_element_type=jnp.float32,
    )


def whitening(gram, count):
    width = gram.shape[0]
    identity = jnp.eye(width, dtype=jnp.float32)
    shifted = gram + 1e-05 * jnp.trace(gram) / width * identity
    lower = jnp.linalg.cholesky(shifted)
    inverse = jax.scipy.linalg.solve_triangular(lower, identity, lower=True)
    return jnp.transpose(inverse) * math.sqrt(count)


def transposed_product(left, right):
    return lax.dot_general(
        left, right, (((0,), (0,)), ((), ())), preferred_element_type=jnp.float32
    )


def loading_total(partial_sum, gene_scale):
    return total_of(partial_sum, "cells") * gene_scale


def shards(counts, sketch):
    cell_dev, gene_dev = counts.shape
    group_count = lax.axis_size("genes")
    cell_count = float(cell_dev * lax.axis_size("cells"))
    gene_count = float(gene_dev * group_count)
    cell_part = jnp.sum(counts, axis=1).astype(jnp.float32)
    gene_part = jnp.sum(counts, axis=0).astype(jnp.float32)
    gene_total, group_sum = in_one((gene_part, jnp.sum(gene_part)), "cells")
    cell_total, grand = in_one((cell_part, group_sum), "genes")
    frac = gene_total / grand
    limit = math.sqrt(cell_count)
    resid = residual_block(counts, cell_total, frac, limit)
    gene_scale = math.sqrt(gene_count) / cell_count
    omega = sketch
    basis = None
    loadings = None
    for sweep in range(ITERS):
        sketched = lax.psum(jnp.dot(resid, omega, preferred_element_type=jnp.float32), "genes")
        gram = total_of_2(self_gram(sketched), "cells")
        basis = jnp.dot(sketched, whitening(gram, cell_count), precision=lax.Precision.HIGHEST)
        partial_sum = transposed_product(resid, basis.astype(jnp.bfloat16))
        loadings = loading_total(partial_sum, gene_scale)
        if sweep < ITERS - 1:
            omega = loadings.astype(jnp.bfloat16)
    return (basis, loadings)


def solution(mesh):
    return jax.shard_map(
        shards,
        mesh=mesh,
        in_specs=(P("cells", "genes"), P("genes", None)),
        out_specs=(P("cells", None), P("genes", None)),
        check_vma=False,
    )
```

profile of v0, /device:TPU:32, one launch (start us, length us, event | category | flops | bytes accessed | tf_op | source)
XLA Modules:
  0.0 410.6 jit_solution(17012000209394934699)
XLA Ops:
  7.2 4.7 %fusion.14 = (s32[4864]{0:T(1024)S(1)}, s32[500]{0:T(512)S(1)}) fusion(s32[4864,500]{0,1:T(8,128)} %param.5), kind=kLoop, calls=%fused_computation.44 | loop fusion | flops 4858636 | bytes 9749456 | tf_op jit(solution)/shard_map/reduce_sum | solution.py:112
  13.8 11.2 %all-to-all-start = ((f32[32,1,501]{2,1,0:T(1,128)}), f32[32,1,501]{2,1,0:T(1,128)S(1)}, u32[]{:S(2)}, u32[]{:S(2)}) async-start(f32[32,1,501]{2,1,0:T(1,128)} %broadcast_in_dim.26), calls=%async_computation | async-start | bytes 131072 | tf_op jit(solution)/shard_map/all_to_all | solution.py:20
  25.1 9.0 %all-to-all-done = f32[32,1,501]{2,1,0:T(1,128)S(1)} async-done(((f32[32,1,501]{2,1,0:T(1,128)}), f32[32,1,501]{2,1,0:T(1,128)S(1)}, u32[]{:S(2)}, u32[]{:S(2)}) %all-to-all-start) | async-done | bytes 64160 | tf_op jit(solution)/shard_map/all_to_all | solution.py:20
  35.5 10.7 %all_to_all.64 = f32[8,1,4865]{2,1,0:T(1,128)S(1)} all-to-all(f32[8,1,4865]{2,1,0:T(1,128)S(1)} %broadcast_in_dim.27), channel_id=1, replica_groups=mesh['cells'=32,'genes'=8] {'genes'}, dimensions={0} | all-to-all | bytes 311360 | tf_op jit(solution)/shard_map/all_to_all | solution.py:20
  47.4 6.0 %fusion.2 = bf16[4864,500]{0,1:T(8,128)(2,1)S(1)} fusion(s32[4864,500]{0,1:T(8,128)} %param.5, f32[500]{0:T(512)S(1)} %slice_divide_fusion, f32[4864]{0:T(1024)S(1)} %bitcast.44), kind=kLoop, calls=%fused_computation.6 | loop fusion | flops 21888000 | bytes 14613456 | tf_op jit(solution)/shard_map/convert_element_type | solution.py:75
  58.7 65.9 %all-reduce.3.cloned.1.call-done = f32[4864,128]{1,0:T(8,128)} async-done(((f32[4864,128]{1,0:T(8,128)}), f32[4864,128]{1,0:T(8,128)}) %all-reduce.3.cloned.1.call-update) | async-done | bytes 2490384 | tf_op jit(solution)/shard_map/psum | solution.py:124
  124.6 6.7 %fusion.16 = f32[128,128]{1,0:T(8,128)S(1)} fusion(f32[4864,128]{1,0:T(8,128)} %all-reduce.3.cloned.1.call-done), kind=kOutput, calls=%fused_computation.46 | convolution fusion | flops 956301312 | bytes 2555904 | tf_op jit(solution)/shard_map/dot_general | solution.py:79
  131.3 18.9 %all_to_all.65 = f32[32,4,128]{2,1,0:T(4,128)S(1)} all-to-all(f32[32,4,128]{2,1,0:T(4,128)S(1)} %bitcast.42), channel_id=1, replica_groups=mesh['cells'=32,'genes'=8] {'cells'}, dimensions={0} | all-to-all | bytes 131072 | tf_op jit(solution)/shard_map/all_to_all | solution.py:41
  150.8 4.7 %all-to-all-start.3 = ((f32[32,4,128]{2,1,0:T(4,128)}), f32[32,4,128]{2,1,0:T(4,128)S(1)}, u32[]{:S(2)}, u32[]{:S(2)}) async-start(f32[32,4,128]{2,1,0:T(4,128)} %broadcast_in_dim.28), calls=%async_computation.3 | async-start | bytes 131072 | tf_op jit(solution)/shard_map/all_to_all | solution.py:20
  155.8 8.8 %all-to-all-done.3 = f32[32,4,128]{2,1,0:T(4,128)S(1)} async-done(((f32[32,4,128]{2,1,0:T(4,128)}), f32[32,4,128]{2,1,0:T(4,128)S(1)}, u32[]{:S(2)}, u32[]{:S(2)}) %all-to-all-start.3) | async-done | bytes 65568 | tf_op jit(solution)/shard_map/all_to_all | solution.py:20
  166.2 11.7 %cholesky.44 = f32[128,128]{1,0:T(8,128)S(1)} custom-call(f32[128,128]{1,0:T(8,128)S(1)} %fusion.13), custom_call_target="Cholesky" | custom-call | tf_op jit(solution)/shard_map/jit(cholesky)/cholesky | solution.py:92
  179.3 9.8 %custom-call.6 = f32[1,128,128]{1,2,0:T(8,128)S(1)} custom-call(f32[1,128,128]{2,1,0:T(8,128)S(1)} %fusion.8), custom_call_target="InvertDiagBlocksLowerTriangular" | custom-call | tf_op jit(solution)/shard_map/jit(_solve_triangular)/triangular_solve | solution.py:93
  195.7 14.9 %all_to_all.66 = f32[32,1,2000]{2,1,0:T(1,128)S(1)} all-to-all(f32[32,1,2000]{2,1,0:T(1,128)S(1)} %all_to_all.52), channel_id=1, replica_groups=mesh['cells'=32,'genes'=8] {'cells'}, dimensions={0} | all-to-all | bytes 512000 | tf_op jit(solution)/shard_map/all_to_all | solution.py:41
  210.9 15.4 %all_to_all.67 = f32[32,1,2000]{2,1,0:T(1,128)S(1)} all-to-all(f32[32,1,2000]{2,1,0:T(1,128)S(1)} %broadcast_in_dim.30), channel_id=1, replica_groups=mesh['cells'=32,'genes'=8] {'cells'}, dimensions={0} | all-to-all | bytes 512000 | tf_op jit(solution)/shard_map/all_to_all | solution.py:20
  227.3 5.3 %fusion.18 = f32[4864,128]{1,0:T(8,128)} fusion(bf16[4864,500]{0,1:T(8,128)(2,1)} %copy-done.1, bf16[500,128]{1,0:T(8,128)(2,1)S(1)} %convert_element_type.37), kind=kOutput, calls=%fused_computation.48 | convolution fusion | flops 622592000 | bytes 7482368 | tf_op jit(solution)/shard_map/dot_general | solution.py:124
  232.7 67.0 %all-reduce.5.cloned.1.call-done = f32[4864,128]{1,0:T(8,128)} async-done(((f32[4864,128]{1,0:T(8,128)}), f32[4864,128]{1,0:T(8,128)}) %all-reduce.5.cloned.1.call-update) | async-done | bytes 2490384 | tf_op jit(solution)/shard_map/psum | solution.py:124
  299.7 6.7 %fusion.19 = f32[128,128]{1,0:T(8,128)S(1)} fusion(f32[4864,128]{1,0:T(8,128)} %all-reduce.5.cloned.1.call-done), kind=kOutput, calls=%fused_computation.49 | convolution fusion | flops 956301312 | bytes 2555904 | tf_op jit(solution)/shard_map/dot_general | solution.py:79
  306.4 18.9 %all_to_all.68 = f32[32,4,128]{2,1,0:T(4,128)S(1)} all-to-all(f32[32,4,128]{2,1,0:T(4,128)S(1)} %bitcast.43), channel_id=1, replica_groups=mesh['cells'=32,'genes'=8] {'cells'}, dimensions={0} | all-to-all | bytes 131072 | tf_op jit(solution)/shard_map/all_to_all | solution.py:41
  325.3 13.3 %all_to_all.69 = f32[32,4,128]{2,1,0:T(4,128)S(1)} all-to-all(f32[32,4,128]{2,1,0:T(4,128)S(1)} %broadcast_in_dim.31), channel_id=1, replica_groups=mesh['cells'=32,'genes'=8] {'cells'}, dimensions={0} | all-to-all | bytes 131072 | tf_op jit(solution)/shard_map/all_to_all | solution.py:20
  340.2 11.7 %cholesky.55 = f32[128,128]{1,0:T(8,128)S(1)} custom-call(f32[128,128]{1,0:T(8,128)S(1)} %fusion.11), custom_call_target="Cholesky" | custom-call | tf_op jit(solution)/shard_map/jit(cholesky)/cholesky | solution.py:92
  353.3 9.8 %custom-call.7 = f32[1,128,128]{1,2,0:T(8,128)S(1)} custom-call(f32[1,128,128]{2,1,0:T(8,128)S(1)} %fusion.9), custom_call_target="InvertDiagBlocksLowerTriangular" | custom-call | tf_op jit(solution)/shard_map/jit(_solve_triangular)/triangular_solve | solution.py:93
  367.0 3.9 fusion.4
  371.3 14.9 %all_to_all.70 = f32[32,1,2000]{2,1,0:T(1,128)S(1)} all-to-all(f32[32,1,2000]{2,1,0:T(1,128)S(1)} %all_to_all.53), channel_id=1, replica_groups=mesh['cells'=32,'genes'=8] {'cells'}, dimensions={0} | all-to-all | bytes 512000 | tf_op jit(solution)/shard_map/all_to_all | solution.py:41
  386.4 15.2 %all_to_all.71 = f32[32,1,2000]{2,1,0:T(1,128)S(1)} all-to-all(f32[32,1,2000]{2,1,0:T(1,128)S(1)} %broadcast_in_dim.32), channel_id=1, replica_groups=mesh['cells'=32,'genes'=8] {'cells'}, dimensions={0} | all-to-all | bytes 512000 | tf_op jit(solution)/shard_map/all_to_all | solution.py:20
  (63 shorter events, 29.6 us)
Async XLA Ops:
  7.2 48.5 %copy-start = (bf16[500,128]{1,0:T(8,128)(2,1)S(1)}, bf16[500,128]{1,0:T(8,128)(2,1)}, u32[]{:S(2)}) copy-start(bf16[500,128]{1,0:T(8,128)(2,1)} %param.6) | copy-start | bytes 384004
  13.8 20.2 %all-to-all-start = ((f32[32,1,501]{2,1,0:T(1,128)}), f32[32,1,501]{2,1,0:T(1,128)S(1)}, u32[]{:S(2)}, u32[]{:S(2)}) async-start(f32[32,1,501]{2,1,0:T(1,128)} %broadcast_in_dim.26), calls=%async_computation | async-start | bytes 131072 | tf_op jit(solution)/shard_map/all_to_all | solution.py:20
  25.0 99.6 %all-reduce.3.cloned.1.call-start = ((), (), s32[]{:S(2)}) async-start(), calls=%async_computation.10 | async-start | bytes 4980736 | tf_op jit(solution)/shard_map/psum | solution.py:124
  53.5 2.2 copy-start.1
  124.6 64.8 %copy-start.3 = (f32[4864,128]{1,0:T(8,128)S(1)}, f32[4864,128]{1,0:T(8,128)}, u32[]{:S(2)}) copy-start(f32[4864,128]{1,0:T(8,128)} %all-reduce.3.cloned.1.call-done) | copy-start | bytes 7471108
  150.8 13.8 %all-to-all-start.3 = ((f32[32,4,128]{2,1,0:T(4,128)}), f32[32,4,128]{2,1,0:T(4,128)S(1)}, u32[]{:S(2)}, u32[]{:S(2)}) async-start(f32[32,4,128]{2,1,0:T(4,128)} %broadcast_in_dim.28), calls=%async_computation.3 | async-start | bytes 131072 | tf_op jit(solution)/shard_map/all_to_all | solution.py:20
  155.5 144.2 %all-reduce.5.cloned.1.call-start = ((), (), s32[]{:S(2)}) async-start(), calls=%async_computation.11 | async-start | bytes 4980736 | tf_op jit(solution)/shard_map/psum | solution.py:124
  299.7 63.7 %copy-start.2 = (f32[4864,128]{1,0:T(8,128)S(1)}, f32[4864,128]{1,0:T(8,128)}, u32[]{:S(2)}) copy-start(f32[4864,128]{1,0:T(8,128)} %all-reduce.5.cloned.1.call-done) | copy-start | bytes 7471108
  365.6 1.5 copy-start.4
Sparse Core Ops, SparseCore 0:
  58.8 65.7 all-reduce.2
  232.8 66.8 all-reduce.4
where the time goes:
time: 418 us; the launch traced here: 411 us
  waiting for transfers between devices  151 us (36%)
  blocking collectives  122 us (29%)
  other arithmetic  62.7 us (15%)
  matrix products  34.2 us (8%)
  starting transfers between devices  16.2 us (4%)
  between operations  16.1 us (4%)
  local copies, waits for them, and re-layouts  8.66 us (2%)
    psum x2, waiting for transfers between devices, shards(): lax.psum(jnp.dot(resid, omega, preferred_element_type=jnp.float32), 'genes')  133 us
    all_to_all x4, blocking collectives, summed_on_arrival(): parts = lax.all_to_all(split_up(array, dim, size), axis, 0, 0, tiled=True)  67.5 us
    all_to_all x4, blocking collectives, from_everyone(): return lax.all_to_all(copies, axis, split_axis=0, concat_axis=0, tiled=True)  54.5 us
    another operation x6, other arithmetic, whitening(): lower = jnp.linalg.cholesky(shifted)  24.8 us
    another operation x4, other arithmetic, whitening(): inverse = jax.scipy.linalg.solve_triangular(lower, identity, lower=True)  20.9 us
    all_to_all x2, waiting for transfers between devices, from_everyone(): return lax.all_to_all(copies, axis, split_axis=0, concat_axis=0, tiled=True)  17.8 us
    all_to_all x2, starting transfers between devices, from_everyone(): return lax.all_to_all(copies, axis, split_axis=0, concat_axis=0, tiled=True)  15.9 us
    dot_general x2, matrix products, self_gram(): lax.dot_general(block, block, (((0,), (0,)), ((), ())), precision=lax.Pre...  13.3 us
  transfers between devices with their start and end apart: 4, of which 4 were waited for; matrix products, arithmetic and copies ran while one was open for 0% of the time, Pallas kernels for 0%

commit v1 on v0

v1 whole, which is shorter than its diff:
```python
import functools
import math

import jax
import jax.numpy as jnp
from jax import lax
from jax.experimental import pallas as pl
from jax.experimental.pallas import tpu as pltpu
from jax.sharding import PartitionSpec as P

ITERS = 2
NX = 4
NK = 2
TILE = 128
STEP = 32
PANEL = 8
HIGHEST = lax.Precision.HIGHEST
MESH = pl.DeviceIdType.MESH
F32 = jnp.float32
BF16 = jnp.bfloat16


def outer_contract(left, right, precision=None):
    return lax.dot_general(
        left, right, (((0,), (0,)), ((), ())), precision=precision, preferred_element_type=F32
    )


def kernel(
    dims,
    counts_hbm,
    sketch_ref,
    s_out,
    w_out,
    load_out,
    cnt,
    res,
    ct,
    cellx,
    totc,
    genex,
    genez,
    grp,
    fracs,
    omega,
    psend,
    precv,
    pown,
    qbuf,
    fbuf,
    rbuf,
    sfull,
    tacc,
    gacc,
    txs,
    txr,
    tzs,
    tzr,
    tall,
    gx,
    gz,
    gg,
    aug,
    linv,
    load_sem,
    out_sem,
    bx_ss,
    bx_rs,
    bz_ss,
    bz_rs,
    ba_ss,
    ba_rs,
    bg_ss,
    bg_rs,
    pr_ss,
    pr_rs,
    f_ss,
    f_rs,
    r_ss,
    r_rs,
    ag_ss,
    ag_rs,
    tx_ss,
    tx_rs,
    tz_ss,
    tz_rs,
    taz_ss,
    taz_rs,
    tax_ss,
    tax_rs,
    gx_ss,
    gx_rs,
    gz_ss,
    gz_rs,
    gg_ss,
    gg_rs,
):
    nx, nz, ng, rows, genes, wide, rank, n_cells, n_genes = dims
    ny = ng // NK
    shard = rows // ng
    half = shard // 2
    tiles = rows // TILE
    blk = wide // nx
    zr = rank // nz
    gr = rank // ng
    me_c = lax.axis_index("cells")
    me_g = lax.axis_index("genes")
    mz, mx = me_c // nx, lax.rem(me_c, nx)
    my, mk = me_g // NK, lax.rem(me_g, NK)
    ok = 1 - mk
    y_up, y_dn, y_far = (lax.rem(my + d, ny) for d in (1, 3, 2))

    def copy(src, dst, ss, rs, c, g):
        return pltpu.make_async_remote_copy(
            src_ref=src, dst_ref=dst, send_sem=ss, recv_sem=rs, device_id=(c, g), device_id_type=MESH
        )

    def x_peer(i):
        return mz * nx + i, me_g

    def z_peer(i):
        return i * nx + mx, me_g

    def g_peer(i):
        return me_c, i

    sent = []

    def spread(n, me, peer, src_of, dst, ss, rs):
        arrivals = []
        for d in range(1, n):
            to, frm = lax.rem(me + d, n), lax.rem(me + n - d, n)
            out = copy(src_of(to), dst.at[me], ss.at[d], rs.at[d], *peer(to))
            out.start()
            sent.append(out)
            arrivals.append(copy(src_of(to), dst.at[frm], ss.at[d], rs.at[d], *peer(to)))
        return arrivals

    def wait_all(arrivals):
        for a in arrivals:
            a.wait_recv()

    def total(slots, n):
        acc = slots[0]
        for i in range(1, n):
            acc = acc + slots[i]
        return acc

    barrier = pltpu.get_barrier_semaphore()
    for n, me, peer in ((nx, mx, x_peer), (nz, mz, z_peer), (ng, me_g, g_peer)):
        for d in range(1, n):
            pl.semaphore_signal(barrier, inc=1, device_id=peer(lax.rem(me + d, n)), device_id_type=MESH)

    per = 2 * TILE if tiles % 2 == 0 else TILE
    loads = []
    for i in range(rows // per):
        part = pl.ds(i * per, per)
        loads.append(pltpu.make_async_copy(counts_hbm.at[part], cnt.at[part], load_sem.at[i]))
        loads[-1].start()

    omega[pl.ds(wide - TILE, TILE), :] = jnp.zeros((TILE, rank), BF16)
    omega[pl.ds(0, genes), :] = sketch_ref[...]

    groups = wide // TILE
    spare = wide - genes

    def lanes(r, n):
        out = []
        for g in range(groups):
            if g < groups - 1:
                out.append(cnt[pl.ds(r, n), pl.ds(g * TILE, TILE)].astype(F32))
            else:
                last = cnt[pl.ds(r, n), pl.ds(g * TILE, TILE - spare)].astype(F32)
                out.append(jnp.concatenate([last, jnp.zeros((n, spare), F32)], axis=1))
        return out

    cols = tuple(jnp.zeros((8, TILE), F32) for _ in range(groups))
    sub = per // TILE

    def stats(i, cols):
        part = pl.ds(pl.multiple_of(i * per, per), per)
        pltpu.make_async_copy(counts_hbm.at[part], cnt.at[part], load_sem.at[i]).wait()
        for j in range(sub):
            xs = lanes(pl.multiple_of(i * per + j * TILE, TILE), TILE)
            cols = tuple(c + jnp.sum(x.reshape(TILE // 8, 8, TILE), axis=0) for c, x in zip(cols, xs))
            line = xs[0]
            for x in xs[1:]:
                line = line + x
            across = jnp.sum(jnp.transpose(line), axis=0, keepdims=True)
            cellx[me_g, pl.ds(i * sub + j, 1), :] = across
        return cols

    cols = lax.fori_loop(0, rows // per, stats, cols)
    for g in range(groups):
        genex[mx, :, pl.ds(g * TILE, TILE)] = jnp.sum(cols[g], axis=0, keepdims=True)

    pl.semaphore_wait(barrier, nx + nz + ng - 3)
    got_x = spread(nx, mx, x_peer, lambda to: genex.at[mx], genex, bx_ss, bx_rs)
    got_a = spread(ng, me_g, g_peer, lambda to: cellx.at[me_g], cellx, ba_ss, ba_rs)
    wait_all(got_x)
    genez[mz] = total(genex, nx)
    got_z = spread(nz, mz, z_peer, lambda to: genez.at[mz], genez, bz_ss, bz_rs)
    wait_all(got_a)
    totc[...] = total(cellx, ng)

    def widen(t, carry):
        line = jnp.broadcast_to(totc[pl.ds(t, 1), :], (TILE, TILE))
        ct[pl.ds(pl.multiple_of(t * TILE, TILE), TILE), :] = jnp.transpose(line)
        return carry

    lax.fori_loop(0, tiles, widen, 0)
    wait_all(got_z)
    gene_total = total(genez, nz)
    short = gene_total[:, :TILE]
    for g in range(1, groups):
        short = short + gene_total[:, g * TILE : (g + 1) * TILE]
    grp[me_g] = short
    wait_all(spread(ng, me_g, g_peer, lambda to: grp.at[me_g], grp, bg_ss, bg_rs))
    grand = jnp.sum(total(grp, ng), axis=1, keepdims=True)
    fill = lax.broadcasted_iota(jnp.int32, (1, wide), 1) >= genes
    fracs[...] = jnp.where(fill, 1.0, gene_total / grand)

    limit = math.sqrt(n_cells)

    def residuals(base):
        def some(i, carry):
            r = pl.multiple_of(base + i * STEP, STEP)
            cell = ct[pl.ds(r, STEP), :]
            xs = lanes(r, STEP)
            for g in range(groups):
                mu = cell * fracs[:, pl.ds(g * TILE, TILE)]
                value = (xs[g] - mu) * lax.rsqrt(mu + 0.01 * mu * mu)
                value = jnp.clip(value, -limit, limit)
                if g == groups - 1:
                    lane = lax.broadcasted_iota(jnp.int32, (STEP, TILE), 1)
                    value = jnp.where(lane < TILE - spare, value, 0.0)
                res[pl.ds(r, STEP), pl.ds(g * TILE, TILE)] = value.astype(BF16)
            return carry

        lax.fori_loop(0, shard // STEP, some, 0)

    gene_scale = math.sqrt(n_genes) / n_cells

    def whiten(it):
        eye = (
            lax.broadcasted_iota(jnp.int32, (rank, rank), 0)
            == lax.broadcasted_iota(jnp.int32, (rank, rank), 1)
        )
        gram = jnp.concatenate([gg[it, i] for i in range(ng)], axis=0)
        diagonal = jnp.sum(jnp.sum(jnp.where(eye, gram, 0.0), axis=1, keepdims=True), axis=0, keepdims=True)
        aug[:, pl.ds(0, rank)] = gram + jnp.where(eye, 1e-05 * diagonal / rank, 0.0)
        aug[:, pl.ds(rank, rank)] = jnp.where(eye, 1.0, 0.0)
        lane = lax.broadcasted_iota(jnp.int32, (PANEL, rank), 1)
        row = lax.broadcasted_iota(jnp.int32, (PANEL, 2 * rank), 0)

        def panel(p, carry):
            j = pl.multiple_of(p * PANEL, PANEL)
            lines = aug[pl.ds(j, PANEL), :]
            left = lines[:, :rank]
            heads = [
                jnp.sum(jnp.where(lane == j + i, left, 0.0), axis=1, keepdims=True) for i in range(PANEL)
            ]
            for i in range(PANEL):
                inv = lax.rsqrt(heads[i][i : i + 1, :])
                col = heads[i] * inv
                for m in range(i + 1, PANEL):
                    heads[m] = heads[m] - col * col[m : m + 1, :]
                this = lines[i : i + 1, :] * inv
                lines = jnp.where(row > i, lines - col * this, jnp.where(row == i, this, lines))
            linv[pl.ds(j, PANEL), :] = lines[:, rank:]
            aug[...] = aug[...] - outer_contract(lines[:, :rank], lines, HIGHEST)
            return carry

        lax.fori_loop(0, rank // PANEL, panel, 0)
        return jnp.transpose(linv[...]) * math.sqrt(n_cells)

    for it in range(ITERS):
        order = (y_far, y_up, y_dn, my)

        def pair(n):
            for k in (ok, mk):
                base = pl.multiple_of((order[n] * NK + k) * shard, 16)
                if it == 0:
                    residuals(base)
                part = jnp.dot(res[pl.ds(base, shard), :], omega[...], preferred_element_type=F32)
                if k is ok:
                    psend[it, n] = part
                    out = copy(
                        psend.at[it, n], precv.at[it, n], pr_ss.at[it, n], pr_rs.at[it, n], *g_peer(my * NK + ok)
                    )
                    out.start()
                    sent.append(out)
                else:
                    pown[n] = part

        def both(n):
            copy(
                psend.at[it, n], precv.at[it, n], pr_ss.at[it, n], pr_rs.at[it, n], *g_peer(my * NK + ok)
            ).wait_recv()
            return pown[n] + precv[it, n]

        up, dn = g_peer(y_up * NK + mk), g_peer(y_dn * NK + mk)
        other = g_peer(my * NK + ok)
        top, bot = pl.ds(0, half), pl.ds(half, half)

        pair(0)
        pair(1)
        qbuf[it, 0] = both(0).astype(BF16)
        far_up = copy(qbuf.at[it, 0, top], fbuf.at[it, 0], f_ss.at[it, 0], f_rs.at[it, 0], *up)
        far_dn = copy(qbuf.at[it, 0, bot], fbuf.at[it, 1], f_ss.at[it, 1], f_rs.at[it, 1], *dn)
        far_up.start()
        far_dn.start()
        pair(2)
        q = both(1)
        far_up.wait_recv()
        qbuf[it, 1, top] = (q[:half] + fbuf[it, 0].astype(F32)).astype(BF16)
        qbuf[it, 1, bot] = q[half:].astype(BF16)
        near_up = copy(qbuf.at[it, 1], rbuf.at[it, 0], r_ss.at[it, 0], r_rs.at[it, 0], *up)
        near_up.start()
        q = both(2)
        far_dn.wait_recv()
        qbuf[it, 2, top] = q[:half].astype(BF16)
        qbuf[it, 2, bot] = (q[half:] + fbuf[it, 1].astype(F32)).astype(BF16)
        near_dn = copy(qbuf.at[it, 2], rbuf.at[it, 1], r_ss.at[it, 1], r_rs.at[it, 1], *dn)
        near_dn.start()
        pair(3)
        own = both(3)
        near_up.wait_recv()
        near_dn.wait_recv()
        sfull[it, me_g] = (own + rbuf[it, 0].astype(F32) + rbuf[it, 1].astype(F32)).astype(BF16)
        sent.extend([far_up, far_dn, near_up, near_dn])

        def block(g, part=None):
            return sfull.at[it, g] if part is None else sfull.at[it, g, part]

        def send(n, g, part, peer):
            out = copy(block(g, part), block(g, part), ag_ss.at[it, n], ag_rs.at[it, n], *peer)
            out.start()
            sent.append(out)

        def arrive(n, g, part):
            copy(block(g, part), block(g, part), ag_ss.at[it, n], ag_rs.at[it, n], *other).wait_recv()

        mine = me_g
        up_k, dn_k, far_k = (y * NK + mk for y in (y_up, y_dn, y_far))
        up_o, dn_o, far_o = (y * NK + ok for y in (y_up, y_dn, y_far))
        mine_o = my * NK + ok

        def gather(first, g):
            base = pl.multiple_of(g * shard, 16)
            s = sfull[it, g]
            t = outer_contract(s, res[pl.ds(base, shard), :])
            u = outer_contract(s, s)
            if first:
                tacc[it] = t
                gacc[it] = u
            else:
                tacc[it] = tacc[it] + t
                gacc[it] = gacc[it] + u

        send(0, mine, top, up)
        send(1, mine, bot, dn)
        send(2, mine, bot, up)
        send(3, mine, top, dn)
        send(4, mine, None, other)
        gather(True, mine)
        arrive(0, dn_k, top)
        send(5, dn_k, top, up)
        arrive(1, up_k, bot)
        send(6, up_k, bot, dn)
        arrive(4, mine_o, None)
        gather(False, mine_o)
        arrive(2, dn_k, bot)
        send(7, dn_k, None, other)
        arrive(3, up_k, top)
        send(8, up_k, None, other)
        gather(False, dn_k)
        gather(False, up_k)
        arrive(7, dn_o, None)
        gather(False, dn_o)
        arrive(8, up_o, None)
        gather(False, up_o)
        arrive(5, far_k, top)
        arrive(6, far_k, bot)
        send(9, far_k, None, other)
        gather(False, far_k)
        arrive(9, far_o, None)
        gather(False, far_o)
        if it == ITERS - 1:
            leave = pltpu.make_async_copy(sfull.at[it], s_out, out_sem)
            leave.start()

        for i in range(nx):
            txs[it, i] = tacc[it, :, pl.ds(i * blk, blk)]
        txr[it, mx] = txs[it, mx]
        gx[it, mx] = gacc[it, pl.ds(pl.multiple_of(me_g * gr, 8), gr), :]
        got_gx = spread(nx, mx, x_peer, lambda to: gx.at[it, mx], gx.at[it], gx_ss.at[it], gx_rs.at[it])
        got_tx = spread(nx, mx, x_peer, lambda to: txs.at[it, to], txr.at[it], tx_ss.at[it], tx_rs.at[it])
        wait_all(got_gx)
        gz[it, mz] = total([gx[it, i] for i in range(nx)], nx)
        got_gz = spread(nz, mz, z_peer, lambda to: gz.at[it, mz], gz.at[it], gz_ss.at[it], gz_rs.at[it])
        wait_all(got_tx)
        tsum = total([txr[it, i] for i in range(nx)], nx)
        for i in range(nz):
            tzs[it, i] = tsum[i * zr : (i + 1) * zr, :]
        tzr[it, mz] = tzs[it, mz]
        got_tz = spread(nz, mz, z_peer, lambda to: tzs.at[it, to], tzr.at[it], tz_ss.at[it], tz_rs.at[it])
        wait_all(got_gz)
        gg[it, me_g] = total([gz[it, i] for i in range(nz)], nz)
        got_gg = spread(ng, me_g, g_peer, lambda to: gg.at[it, me_g], gg.at[it], gg_ss.at[it], gg_rs.at[it])
        wait_all(got_tz)
        tall[it, mx, mz] = total([tzr[it, i] for i in range(nz)], nz)
        got_taz = spread(
            nz, mz, z_peer, lambda to: tall.at[it, mx, mz], tall.at[it, mx], taz_ss.at[it], taz_rs.at[it]
        )
        wait_all(got_gg)
        white = whiten(it)
        wait_all(got_taz)
        got_tax = spread(
            nx, mx, x_peer, lambda to: tall.at[it, mx], tall.at[it], tax_ss.at[it], tax_rs.at[it]
        )
        if it == ITERS - 1:
            w_out[...] = white
        wait_all(got_tax)
        for i in range(nx):
            t = jnp.concatenate([tall[it, i, j] for j in range(nz)], axis=0)
            loading = outer_contract(t, white, HIGHEST) * gene_scale
            if it == ITERS - 1:
                load_out[pl.ds(i * blk, blk), :] = loading
            else:
                omega[pl.ds(i * blk, blk), :] = loading.astype(BF16)

    leave.wait()
    for s in sent:
        s.wait_send()


def shards(counts, sketch):
    rows, genes = counts.shape
    rank = sketch.shape[1]
    nc, ng = lax.axis_size("cells"), lax.axis_size("genes")
    nx = NX
    nz = nc // nx
    wide = -(-genes // TILE) * TILE
    shard = rows // ng
    tiles = rows // TILE
    blk, zr, gr = wide // nx, rank // nz, rank // ng
    dims = (nx, nz, ng, rows, genes, wide, rank, nc * rows, ng * genes)
    per = 2 * TILE if tiles % 2 == 0 else TILE
    V = pltpu.VMEM
    D = pltpu.SemaphoreType.DMA

    def pairs(*shape):
        return [D(shape), D(shape)]

    s_all, white, load = pl.pallas_call(
        functools.partial(kernel, dims),
        out_shape=(
            jax.ShapeDtypeStruct((ng, shard, rank), BF16),
            jax.ShapeDtypeStruct((rank, rank), F32),
            jax.ShapeDtypeStruct((wide, rank), F32),
        ),
        in_specs=[pl.BlockSpec(memory_space=pl.ANY), pl.BlockSpec(memory_space=pltpu.VMEM)],
        out_specs=(
            pl.BlockSpec(memory_space=pl.ANY),
            pl.BlockSpec(memory_space=pltpu.VMEM),
            pl.BlockSpec(memory_space=pltpu.VMEM),
        ),
        scratch_shapes=[
            V((rows, genes), jnp.int32),
            V((rows, wide), BF16),
            V((rows, TILE), F32),
            V((ng, tiles, TILE), F32),
            V((tiles, TILE), F32),
            V((nx, 1, wide), F32),
            V((nz, 1, wide), F32),
            V((ng, 1, TILE), F32),
            V((1, wide), F32),
            V((wide, rank), BF16),
            V((ITERS, 4, shard, rank), F32),
            V((ITERS, 4, shard, rank), F32),
            V((4, shard, rank), F32),
            V((ITERS, 3, shard, rank), BF16),
            V((ITERS, 2, shard // 2, rank), BF16),
            V((ITERS, 2, shard, rank), BF16),
            V((ITERS, ng, shard, rank), BF16),
            V((ITERS, rank, wide), F32),
            V((ITERS, rank, rank), F32),
            V((ITERS, nx, rank, blk), F32),
            V((ITERS, nx, rank, blk), F32),
            V((ITERS, nz, zr, blk), F32),
            V((ITERS, nz, zr, blk), F32),
            V((ITERS, nx, nz, zr, blk), F32),
            V((ITERS, nx, gr, rank), F32),
            V((ITERS, nz, gr, rank), F32),
            V((ITERS, ng, gr, rank), F32),
            V((rank, 2 * rank), F32),
            V((rank, rank), F32),
            D((rows // per,)),
            D,
            *pairs(nx),
            *pairs(nz),
            *pairs(ng),
            *pairs(ng),
            *pairs(ITERS, 4),
            *pairs(ITERS, 2),
            *pairs(ITERS, 2),
            *pairs(ITERS, 10),
            *pairs(ITERS, nx),
            *pairs(ITERS, nz),
            *pairs(ITERS, nz),
            *pairs(ITERS, nx),
            *pairs(ITERS, nx),
            *pairs(ITERS, nz),
            *pairs(ITERS, ng),
        ],
        compiler_params=pltpu.CompilerParams(
            collective_id=0, has_side_effects=True, vmem_limit_bytes=60 * 2**20
        ),
        name="sweep",
    )(counts, sketch)
    basis = jnp.dot(s_all.reshape(rows, rank).astype(F32), white, precision=HIGHEST)
    return basis, load[:genes]


def solution(mesh):
    return jax.shard_map(
        shards,
        mesh=mesh,
        in_specs=(P("cells", "genes"), P("genes", None)),
        out_specs=(P("cells", None), P("genes", None)),
        check_vma=False,
    )
```

time: 418 us -> 141 us (0.34); the launches traced: 411 us -> 138 us
  waiting for transfers between devices: 151 us -> 0 us
  blocking collectives: 122 us -> 0 us
  Pallas kernels: 0 us -> 121 us
  other arithmetic: 62.7 us -> 0 us
  matrix products: 34.2 us -> 3.88 us
  starting transfers between devices: 16.2 us -> 0 us
  between operations: 16.1 us -> 0.64 us
    psum x2 -> x0, waiting for transfers between devices: 133 us -> none  [shards(): lax.psum(jnp.dot(resid, omega, preferred_element_type=jnp.float32), 'genes')]
    all_to_all x8 -> x0, blocking collectives: 122 us -> none  [the longest x4 67.5 us: summed_on_arrival(): parts = lax.all_to_all(split_up(array, dim, size), axis, 0, 0, tiled=True)]
    pallas_call x0 -> x1, Pallas kernels: none -> 121 us  [shards(): pl.pallas_call(functools.partial(kernel, dims), out_shape=(jax.ShapeDtype...]
    another operation x10 -> x0, other arithmetic: 45.7 us -> none  [the longest x6 24.8 us: whitening(): lower = jnp.linalg.cholesky(shifted)]
    dot_general x8 -> x1, matrix products: 33.7 us -> 3.88 us  [shards(): jnp.dot(s_all.reshape(rows, rank).astype(F32), white, precision=HIGHEST)]
    all_to_all x2 -> x0, waiting for transfers between devices: 17.8 us -> none  [from_everyone(): return lax.all_to_all(copies, axis, split_axis=0, concat_axis=0, tiled=True)]
    all_to_all x2 -> x0, starting transfers between devices: 15.9 us -> none  [from_everyone(): return lax.all_to_all(copies, axis, split_axis=0, concat_axis=0, tiled=True)]
    reduce_sum x10 -> x0, other arithmetic: 7.28 us -> none  [the longest x1 4.66 us: shards(): cell_part = jnp.sum(counts, axis=1).astype(jnp.float32)]
  transfers between devices with their start and end apart: 4 -> 0, of which waited for: 4 -> 0; matrix products, arithmetic and copies ran while one was open for 0% -> 0% of each run, Pallas kernels for 0% -> 0%
where the time goes in v1:
time: 141 us; the launch traced here: 138 us
  Pallas kernels  121 us (86%)
  local copies, waits for them, and re-layouts  12.3 us (9%)
  matrix products  3.88 us (3%)
    pallas_call x1, Pallas kernels, shards(): pl.pallas_call(functools.partial(kernel, dims), out_shape=(jax.ShapeDtype...  121 us
    unnamed x1, local copies, waits for them, and re-layouts  10.6 us
    dot_general x1, matrix products, shards(): jnp.dot(s_all.reshape(rows, rank).astype(F32), white, precision=HIGHEST)  3.88 us

profile of v1, /device:TPU:32, one launch (start us, length us, event | category | flops | bytes accessed | tf_op | source)
XLA Modules:
  0.0 138.3 jit_solution(11429222000288603132)
XLA Ops:
  0.6 10.6 %copy.4.counts_hbm = s32[4864,500]{1,0:T(8,128)} copy(s32[4864,500]{0,1:T(8,128)} %param.2) | data formatting | bytes 19456000 | tf_op args[0]
  11.2 121.5 %sweep.1 = (bf16[8,608,128]{2,1,0:T(8,128)(2,1)}, f32[128,128]{1,0:T(8,128)}, f32[512,128]{1,0:T(8,128)}) custom-call(s32[4864,500]{1,0:T(8,128)} %copy.4.counts_hbm, bf16[500,128]{1,0:T(8,128)(2,1)} %sketch_ref.1), custom_call_target="tpu_custom_call" | custom-call | tf_op jit(solution)/shard_map/sweep/pallas_call | solution.py:456
  132.7 1.7 %slice.3 = f32[500,128]{1,0:T(8,128)} slice(f32[512,128]{1,0:T(8,128)} %get-tuple-element.7), slice={[0:500], [0:128]} | slice | bytes 512000 | tf_op jit(solution)/shard_map/slice | solution.py:523
  134.4 3.9 %fusion = f32[4864,128]{1,0:T(8,128)} fusion(bf16[4864,128]{1,0:T(8,128)(2,1)} %bitcast.3, f32[128,128]{1,0:T(8,128)} %get-tuple-element.6), kind=kOutput, calls=%fused_computation | convolution fusion | flops 956301312 | bytes 3801088 | tf_op jit(solution)/shard_map/dot_general | solution.py:522

commit v2 on v1

--- a/solution.py
+++ b/solution.py
@@ -14,6 +14,7 @@
 TILE = 128
 STEP = 32
 PANEL = 8
+PER = 2
 HIGHEST = lax.Precision.HIGHEST
 MESH = pl.DeviceIdType.MESH
 F32 = jnp.float32
@@ -23,6 +24,12 @@
 def outer_contract(left, right, precision=None):
     return lax.dot_general(
         left, right, (((0,), (0,)), ((), ())), precision=precision, preferred_element_type=F32
+    )
+
+
+def inner_contract(left, right, precision=None):
+    return lax.dot_general(
+        left, right, (((1,), (1,)), ((), ())), precision=precision, preferred_element_type=F32
     )
 
 
@@ -35,7 +42,7 @@
     load_out,
     cnt,
     res,
-    ct,
+    gpart,
     cellx,
     totc,
     genex,
@@ -97,11 +104,10 @@
 ):
     nx, nz, ng, rows, genes, wide, rank, n_cells, n_genes = dims
     ny = ng // NK
-    shard = rows // ng
-    half = shard // 2
-    tiles = rows // TILE
+    shard = shard_of(rows, ng)
+    half = rank // 2
     blk = wide // nx
-    zr = rank // nz
+    zr = blk // nz
     gr = rank // ng
     me_c = lax.axis_index("cells")
     me_g = lax.axis_index("genes")
@@ -151,48 +157,45 @@
         for d in range(1, n):
             pl.semaphore_signal(barrier, inc=1, device_id=peer(lax.rem(me + d, n)), device_id_type=MESH)
 
-    per = 2 * TILE if tiles % 2 == 0 else TILE
-    loads = []
-    for i in range(rows // per):
-        part = pl.ds(i * per, per)
-        loads.append(pltpu.make_async_copy(counts_hbm.at[part], cnt.at[part], load_sem.at[i]))
-        loads[-1].start()
-
-    omega[pl.ds(wide - TILE, TILE), :] = jnp.zeros((TILE, rank), BF16)
-    omega[pl.ds(0, genes), :] = sketch_ref[...]
-
+    per = PER * TILE
+    loads = rows // per
+
+    def load(i):
+        part = pl.ds(pl.multiple_of(i * per, TILE), per)
+        return pltpu.make_async_copy(counts_hbm.at[:, part], cnt.at[:, part], load_sem.at[i])
+
+    for i in range(loads):
+        load(i).start()
+
+    res[:, pl.ds(rows, ng * shard - rows)] = jnp.zeros((wide, ng * shard - rows), BF16)
+    flip = jnp.transpose(sketch_ref[...].astype(F32))
+    omega[...] = jnp.concatenate([flip, jnp.zeros((rank, wide - genes), F32)], axis=1).astype(BF16)
+    gpart[...] = jnp.zeros((genes, TILE), jnp.int32)
+    even = genes - genes % 8
+
+    def stats(i, carry):
+        load(i).wait()
+        tot = None
+        for j in range(PER):
+            at = pl.multiple_of(i * per + j * TILE, TILE)
+            x = cnt[:, pl.ds(at, TILE)]
+            tot = x if tot is None else tot + x
+            down = jnp.sum(x[:even].reshape(even // 8, 8, TILE), axis=0)
+            down = jnp.sum(down, axis=0, keepdims=True)
+            if even < genes:
+                down = down + jnp.sum(x[even:], axis=0, keepdims=True)
+            cellx[me_g, :, pl.ds(at, TILE)] = down.astype(F32)
+        gpart[...] = gpart[...] + tot
+        return carry
+
+    lax.fori_loop(0, loads, stats, 0)
     groups = wide // TILE
-    spare = wide - genes
-
-    def lanes(r, n):
-        out = []
-        for g in range(groups):
-            if g < groups - 1:
-                out.append(cnt[pl.ds(r, n), pl.ds(g * TILE, TILE)].astype(F32))
-            else:
-                last = cnt[pl.ds(r, n), pl.ds(g * TILE, TILE - spare)].astype(F32)
-                out.append(jnp.concatenate([last, jnp.zeros((n, spare), F32)], axis=1))
-        return out
-
-    cols = tuple(jnp.zeros((8, TILE), F32) for _ in range(groups))
-    sub = per // TILE
-
-    def stats(i, cols):
-        part = pl.ds(pl.multiple_of(i * per, per), per)
-        pltpu.make_async_copy(counts_hbm.at[part], cnt.at[part], load_sem.at[i]).wait()
-        for j in range(sub):
-            xs = lanes(pl.multiple_of(i * per + j * TILE, TILE), TILE)
-            cols = tuple(c + jnp.sum(x.reshape(TILE // 8, 8, TILE), axis=0) for c, x in zip(cols, xs))
-            line = xs[0]
-            for x in xs[1:]:
-                line = line + x
-            across = jnp.sum(jnp.transpose(line), axis=0, keepdims=True)
-            cellx[me_g, pl.ds(i * sub + j, 1), :] = across
-        return cols
-
-    cols = lax.fori_loop(0, rows // per, stats, cols)
     for g in range(groups):
-        genex[mx, :, pl.ds(g * TILE, TILE)] = jnp.sum(cols[g], axis=0, keepdims=True)
+        n = min(TILE, genes - g * TILE)
+        line = gpart[pl.ds(g * TILE, n), :].astype(F32)
+        if n < TILE:
+            line = jnp.concatenate([line, jnp.zeros((TILE - n, TILE), F32)], axis=0)
+        genex[mx, :, pl.ds(g * TILE, TILE)] = jnp.sum(jnp.transpose(line), axis=0, keepdims=True)
 
     pl.semaphore_wait(barrier, nx + nz + ng - 3)
     got_x = spread(nx, mx, x_peer, lambda to: genex.at[mx], genex, bx_ss, bx_rs)
@@ -202,42 +205,44 @@
     got_z = spread(nz, mz, z_peer, lambda to: genez.at[mz], genez, bz_ss, bz_rs)
     wait_all(got_a)
     totc[...] = total(cellx, ng)
-
-    def widen(t, carry):
-        line = jnp.broadcast_to(totc[pl.ds(t, 1), :], (TILE, TILE))
-        ct[pl.ds(pl.multiple_of(t * TILE, TILE), TILE), :] = jnp.transpose(line)
-        return carry
-
-    lax.fori_loop(0, tiles, widen, 0)
     wait_all(got_z)
     gene_total = total(genez, nz)
     short = gene_total[:, :TILE]
     for g in range(1, groups):
         short = short + gene_total[:, g * TILE : (g + 1) * TILE]
     grp[me_g] = short
-    wait_all(spread(ng, me_g, g_peer, lambda to: grp.at[me_g], grp, bg_ss, bg_rs))
+    got_g = spread(ng, me_g, g_peer, lambda to: grp.at[me_g], grp, bg_ss, bg_rs)
+    fill = lax.broadcasted_iota(jnp.int32, (1, wide), 1) >= genes
+    gene_total = jnp.where(fill, 1.0, gene_total)
+    for g in range(groups):
+        line = jnp.broadcast_to(gene_total[:, g * TILE : (g + 1) * TILE], (TILE, TILE))
+        fracs[pl.ds(g * TILE, TILE), :] = jnp.transpose(line)
+    wait_all(got_g)
     grand = jnp.sum(total(grp, ng), axis=1, keepdims=True)
-    fill = lax.broadcasted_iota(jnp.int32, (1, wide), 1) >= genes
-    fracs[...] = jnp.where(fill, 1.0, gene_total / grand)
+    fracs[...] = fracs[...] / grand
 
     limit = math.sqrt(n_cells)
 
-    def residuals(base):
-        def some(i, carry):
-            r = pl.multiple_of(base + i * STEP, STEP)
-            cell = ct[pl.ds(r, STEP), :]
-            xs = lanes(r, STEP)
-            for g in range(groups):
-                mu = cell * fracs[:, pl.ds(g * TILE, TILE)]
-                value = (xs[g] - mu) * lax.rsqrt(mu + 0.01 * mu * mu)
+    def residuals(g):
+        def some(t, carry):
+            at = pl.ds(pl.multiple_of(t * TILE, TILE), TILE)
+            cell = totc[:, at]
+            for k in range(wide // STEP):
+                n = min(STEP, genes - k * STEP)
+                x = cnt[pl.ds(k * STEP, n), at].astype(F32)
+                if n < STEP:
+                    x = jnp.concatenate([x, jnp.zeros((STEP - n, TILE), F32)], axis=0)
+                mu = cell * fracs[pl.ds(k * STEP, STEP), :]
+                value = (x - mu) * lax.rsqrt(mu + 0.01 * mu * mu)
                 value = jnp.clip(value, -limit, limit)
-                if g == groups - 1:
-                    lane = lax.broadcasted_iota(jnp.int32, (STEP, TILE), 1)
-                    value = jnp.where(lane < TILE - spare, value, 0.0)
-                res[pl.ds(r, STEP), pl.ds(g * TILE, TILE)] = value.astype(BF16)
+                if n < STEP:
+                    row = lax.broadcasted_iota(jnp.int32, (STEP, TILE), 0)
+                    value = jnp.where(row < n, value, 0.0)
+                res[pl.ds(k * STEP, STEP), at] = value.astype(BF16)
             return carry
 
-        lax.fori_loop(0, shard // STEP, some, 0)
+        first = g * (shard // TILE)
+        lax.fori_loop(first, jnp.minimum(first + shard // TILE, rows // TILE), some, 0)
 
     gene_scale = math.sqrt(n_genes) / n_cells
 
@@ -272,17 +277,18 @@
             return carry
 
         lax.fori_loop(0, rank // PANEL, panel, 0)
-        return jnp.transpose(linv[...]) * math.sqrt(n_cells)
+        return linv[...] * math.sqrt(n_cells)
 
     for it in range(ITERS):
         order = (y_far, y_up, y_dn, my)
 
         def pair(n):
             for k in (ok, mk):
-                base = pl.multiple_of((order[n] * NK + k) * shard, 16)
+                g = order[n] * NK + k
+                base = pl.multiple_of(g * shard, TILE)
                 if it == 0:
-                    residuals(base)
-                part = jnp.dot(res[pl.ds(base, shard), :], omega[...], preferred_element_type=F32)
+                    residuals(g)
+                part = jnp.dot(omega[...], res[:, pl.ds(base, shard)], preferred_element_type=F32)
                 if k is ok:
                     psend[it, n] = part
                     out = copy(
@@ -347,10 +353,10 @@
         mine_o = my * NK + ok
 
         def gather(first, g):
-            base = pl.multiple_of(g * shard, 16)
+            base = pl.multiple_of(g * shard, TILE)
             s = sfull[it, g]
-            t = outer_contract(s, res[pl.ds(base, shard), :])
-            u = outer_contract(s, s)
+            t = inner_contract(res[:, pl.ds(base, shard)], s)
+            u = inner_contract(s, s)
             if first:
                 tacc[it] = t
                 gacc[it] = u
@@ -391,7 +397,7 @@
             leave.start()
 
         for i in range(nx):
-            txs[it, i] = tacc[it, :, pl.ds(i * blk, blk)]
+            txs[it, i] = tacc[it, pl.ds(i * blk, blk), :]
         txr[it, mx] = txs[it, mx]
         gx[it, mx] = gacc[it, pl.ds(pl.multiple_of(me_g * gr, 8), gr), :]
         got_gx = spread(nx, mx, x_peer, lambda to: gx.at[it, mx], gx.at[it], gx_ss.at[it], gx_rs.at[it])
@@ -413,26 +419,36 @@
         got_taz = spread(
             nz, mz, z_peer, lambda to: tall.at[it, mx, mz], tall.at[it, mx], taz_ss.at[it], taz_rs.at[it]
         )
-        wait_all(got_gg)
-        white = whiten(it)
         wait_all(got_taz)
         got_tax = spread(
             nx, mx, x_peer, lambda to: tall.at[it, mx], tall.at[it], tax_ss.at[it], tax_rs.at[it]
         )
+        wait_all(got_gg)
+        white = whiten(it)
         if it == ITERS - 1:
             w_out[...] = white
         wait_all(got_tax)
         for i in range(nx):
             t = jnp.concatenate([tall[it, i, j] for j in range(nz)], axis=0)
-            loading = outer_contract(t, white, HIGHEST) * gene_scale
             if it == ITERS - 1:
-                load_out[pl.ds(i * blk, blk), :] = loading
+                load_out[pl.ds(i * blk, blk), :] = inner_contract(t, white, HIGHEST) * gene_scale
             else:
-                omega[pl.ds(i * blk, blk), :] = loading.astype(BF16)
+                omega[:, pl.ds(i * blk, blk)] = (inner_contract(white, t, HIGHEST) * gene_scale).astype(BF16)
 
     leave.wait()
     for s in sent:
         s.wait_send()
+
+
+def shard_of(rows, ng):
+    return -(-rows // (ng * TILE)) * TILE
+
+
+def finish(s_ref, white_ref, load_ref, basis_ref, out_ref):
+    basis_ref[...] = lax.dot_general(
+        s_ref[0].astype(F32), white_ref[...], (((0,), (1,)), ((), ())), precision=HIGHEST, preferred_element_type=F32
+    )
+    out_ref[...] = load_ref[pl.ds(0, out_ref.shape[0]), :]
 
 
 def shards(counts, sketch):
@@ -442,11 +458,10 @@
     nx = NX
     nz = nc // nx
     wide = -(-genes // TILE) * TILE
-    shard = rows // ng
-    tiles = rows // TILE
-    blk, zr, gr = wide // nx, rank // nz, rank // ng
+    shard = shard_of(rows, ng)
+    blk, gr = wide // nx, rank // ng
+    zr = blk // nz
     dims = (nx, nz, ng, rows, genes, wide, rank, nc * rows, ng * genes)
-    per = 2 * TILE if tiles % 2 == 0 else TILE
     V = pltpu.VMEM
     D = pltpu.SemaphoreType.DMA
 
@@ -456,7 +471,7 @@
     s_all, white, load = pl.pallas_call(
         functools.partial(kernel, dims),
         out_shape=(
-            jax.ShapeDtypeStruct((ng, shard, rank), BF16),
+            jax.ShapeDtypeStruct((ng, rank, shard), BF16),
             jax.ShapeDtypeStruct((rank, rank), F32),
             jax.ShapeDtypeStruct((wide, rank), F32),
         ),
@@ -467,36 +482,36 @@
             pl.BlockSpec(memory_space=pltpu.VMEM),
         ),
         scratch_shapes=[
-            V((rows, genes), jnp.int32),
-            V((rows, wide), BF16),
-            V((rows, TILE), F32),
-            V((ng, tiles, TILE), F32),
-            V((tiles, TILE), F32),
+            V((genes, rows), jnp.int32),
+            V((wide, ng * shard), BF16),
+            V((genes, TILE), jnp.int32),
+            V((ng, 1, rows), F32),
+            V((1, rows), F32),
             V((nx, 1, wide), F32),
             V((nz, 1, wide), F32),
             V((ng, 1, TILE), F32),
-            V((1, wide), F32),
-            V((wide, rank), BF16),
-            V((ITERS, 4, shard, rank), F32),
-            V((ITERS, 4, shard, rank), F32),
-            V((4, shard, rank), F32),
-            V((ITERS, 3, shard, rank), BF16),
-            V((ITERS, 2, shard // 2, rank), BF16),
-            V((ITERS, 2, shard, rank), BF16),
-            V((ITERS, ng, shard, rank), BF16),
-            V((ITERS, rank, wide), F32),
+            V((wide, TILE), F32),
+            V((rank, wide), BF16),
+            V((ITERS, 4, rank, shard), F32),
+            V((ITERS, 4, rank, shard), F32),
+            V((4, rank, shard), F32),
+            V((ITERS, 3, rank, shard), BF16),
+            V((ITERS, 2, rank // 2, shard), BF16),
+            V((ITERS, 2, rank, shard), BF16),
+            V((ITERS, ng, rank, shard), BF16),
+            V((ITERS, wide, rank), F32),
             V((ITERS, rank, rank), F32),
-            V((ITERS, nx, rank, blk), F32),
-            V((ITERS, nx, rank, blk), F32),
-            V((ITERS, nz, zr, blk), F32),
-            V((ITERS, nz, zr, blk), F32),
-            V((ITERS, nx, nz, zr, blk), F32),
+            V((ITERS, nx, blk, rank), F32),
+            V((ITERS, nx, blk, rank), F32),
+            V((ITERS, nz, zr, rank), F32),
+            V((ITERS, nz, zr, rank), F32),
+            V((ITERS, nx, nz, zr, rank), F32),
             V((ITERS, nx, gr, rank), F32),
             V((ITERS, nz, gr, rank), F32),
             V((ITERS, ng, gr, rank), F32),
             V((rank, 2 * rank), F32),
             V((rank, rank), F32),
-            D((rows // per,)),
+            D((rows // (PER * TILE),)),
             D,
             *pairs(nx),
             *pairs(nz),
@@ -518,9 +533,25 @@
             collective_id=0, has_side_effects=True, vmem_limit_bytes=60 * 2**20
         ),
         name="sweep",
-    )(counts, sketch)
-    basis = jnp.dot(s_all.reshape(rows, rank).astype(F32), white, precision=HIGHEST)
-    return basis, load[:genes]
+    )(counts.T, sketch)
+    return pl.pallas_call(
+        finish,
+        grid=(-(-rows // shard),),
+        out_shape=(
+            jax.ShapeDtypeStruct((rows, rank), F32),
+            jax.ShapeDtypeStruct((genes, rank), F32),
+        ),
+        in_specs=[
+            pl.BlockSpec((1, rank, shard), lambda i: (i, 0, 0)),
+            pl.BlockSpec((rank, rank), lambda i: (0, 0)),
+            pl.BlockSpec((wide, rank), lambda i: (0, 0)),
+        ],
+        out_specs=(
+            pl.BlockSpec((shard, rank), lambda i: (i, 0)),
+            pl.BlockSpec((genes, rank), lambda i: (0, 0)),
+        ),
+        name="finish",
+    )(s_all, white, load)
 
 
 def solution(mesh):

time: 141 us -> 127 us (0.901); the launches traced: 138 us -> 126 us
  local copies, waits for them, and re-layouts: 12.3 us -> 0 us
  Pallas kernels: 121 us -> 126 us
  matrix products: 3.88 us -> 0 us
    unnamed x1 -> x0, local copies, waits for them, and re-layouts: 10.6 us -> none
    pallas_call x0 -> x1, Pallas kernels: none -> 7.56 us  [shards(): pl.pallas_call(finish, grid=(-(-rows // shard),), out_shape=(jax.ShapeDty...]
    dot_general x1 -> x0, matrix products: 3.88 us -> none  [shards(): jnp.dot(s_all.reshape(rows, rank).astype(F32), white, precision=HIGHEST)]
    pallas_call x1, Pallas kernels: 121 us -> 118 us  [shards(): pl.pallas_call(functools.partial(kernel, dims), out_shape=(jax.ShapeDtype...]
    slice x1 -> x0, local copies, waits for them, and re-layouts: 1.66 us -> none  [shards(): return (basis, load[:genes])]
where the time goes in v2:
time: 127 us; the launch traced here: 126 us
  Pallas kernels  126 us (99%)
    pallas_call x1, Pallas kernels, shards(): pl.pallas_call(functools.partial(kernel, dims), out_shape=(jax.ShapeDtype...  118 us
    pallas_call x1, Pallas kernels, shards(): pl.pallas_call(finish, grid=(-(-rows // shard),), out_shape=(jax.ShapeDty...  7.56 us

profile of v2, /device:TPU:32, one launch (start us, length us, event | category | flops | bytes accessed | tf_op | source)
XLA Modules:
  0.0 126.4 jit_solution(17458764084069831977)
XLA Ops:
  0.6 118.2 %sweep.1 = (bf16[8,128,640]{2,1,0:T(8,128)(2,1)}, f32[128,128]{1,0:T(8,128)}, f32[512,128]{1,0:T(8,128)}) custom-call(s32[500,4864]{1,0:T(8,128)} %bitcast.1, bf16[500,128]{1,0:T(8,128)(2,1)} %sketch_ref.1), custom_call_target="tpu_custom_call" | custom-call | tf_op jit(solution)/shard_map/sweep/pallas_call | solution.py:471
  118.8 7.6 %finish.1 = (f32[4864,128]{1,0:T(8,128)}, f32[500,128]{1,0:T(8,128)}) custom-call(bf16[8,128,640]{2,1,0:T(8,128)(2,1)} %get-tuple-element.5.s_ref, f32[128,128]{1,0:T(8,128)} %get-tuple-element.6.white_ref, f32[512,128]{1,0:T(8,128)} %get-tuple-element.7.load_ref), custom_call_target="tpu_custom_call" | custom-call | tf_op jit(solution)/shard_map/finish/pallas_call | solution.py:537

commit v3 on v2

--- a/solution.py
+++ b/solution.py
@@ -15,6 +15,7 @@
 STEP = 32
 PANEL = 8
 PER = 2
+BLOCKS = 4
 HIGHEST = lax.Precision.HIGHEST
 MESH = pl.DeviceIdType.MESH
 F32 = jnp.float32
@@ -56,14 +57,17 @@
     qbuf,
     fbuf,
     rbuf,
+    late,
     sfull,
+    flat,
     tacc,
-    gacc,
+    gsrc,
+    grow,
     txs,
     txr,
     tzs,
     tzr,
-    tall,
+    oall,
     gx,
     gz,
     gg,
@@ -83,8 +87,6 @@
     pr_rs,
     f_ss,
     f_rs,
-    r_ss,
-    r_rs,
     ag_ss,
     ag_rs,
     tx_ss,
@@ -95,6 +97,8 @@
     taz_rs,
     tax_ss,
     tax_rs,
+    gr_ss,
+    gr_rs,
     gx_ss,
     gx_rs,
     gz_ss,
@@ -105,7 +109,7 @@
     nx, nz, ng, rows, genes, wide, rank, n_cells, n_genes = dims
     ny = ng // NK
     shard = shard_of(rows, ng)
-    half = rank // 2
+    half, quarter = rank // 2, rank // 4
     blk = wide // nx
     zr = blk // nz
     gr = rank // ng
@@ -309,43 +313,50 @@
         other = g_peer(my * NK + ok)
         top, bot = pl.ds(0, half), pl.ds(half, half)
 
+        def hop(src, dst, n, peer):
+            out = copy(src, dst, f_ss.at[it, n], f_rs.at[it, n], *peer)
+            out.start()
+            sent.append(out)
+            return out
+
         pair(0)
         pair(1)
         qbuf[it, 0] = both(0).astype(BF16)
-        far_up = copy(qbuf.at[it, 0, top], fbuf.at[it, 0], f_ss.at[it, 0], f_rs.at[it, 0], *up)
-        far_dn = copy(qbuf.at[it, 0, bot], fbuf.at[it, 1], f_ss.at[it, 1], f_rs.at[it, 1], *dn)
-        far_up.start()
-        far_dn.start()
+        far_up = hop(qbuf.at[it, 0, top], fbuf.at[it, 0], 0, up)
+        far_dn = hop(qbuf.at[it, 0, bot], fbuf.at[it, 1], 1, dn)
+        q = both(1)
+        qbuf[it, 1, bot] = q[half:].astype(BF16)
+        late[0] = q[:half]
+        free_up = hop(qbuf.at[it, 1, bot], rbuf.at[it, 0, bot], 2, up)
         pair(2)
-        q = both(1)
+        q = both(2)
+        qbuf[it, 2, top] = q[:half].astype(BF16)
+        late[1] = q[half:]
+        free_dn = hop(qbuf.at[it, 2, top], rbuf.at[it, 1, top], 3, dn)
+        pair(3)
         far_up.wait_recv()
-        qbuf[it, 1, top] = (q[:half] + fbuf[it, 0].astype(F32)).astype(BF16)
-        qbuf[it, 1, bot] = q[half:].astype(BF16)
-        near_up = copy(qbuf.at[it, 1], rbuf.at[it, 0], r_ss.at[it, 0], r_rs.at[it, 0], *up)
-        near_up.start()
-        q = both(2)
+        qbuf[it, 1, top] = (late[0] + fbuf[it, 0].astype(F32)).astype(BF16)
+        near_up = hop(qbuf.at[it, 1, top], rbuf.at[it, 0, top], 4, up)
         far_dn.wait_recv()
-        qbuf[it, 2, top] = q[:half].astype(BF16)
-        qbuf[it, 2, bot] = (q[half:] + fbuf[it, 1].astype(F32)).astype(BF16)
-        near_dn = copy(qbuf.at[it, 2], rbuf.at[it, 1], r_ss.at[it, 1], r_rs.at[it, 1], *dn)
-        near_dn.start()
-        pair(3)
+        qbuf[it, 2, bot] = (late[1] + fbuf[it, 1].astype(F32)).astype(BF16)
+        near_dn = hop(qbuf.at[it, 2, bot], rbuf.at[it, 1, bot], 5, dn)
         own = both(3)
-        near_up.wait_recv()
-        near_dn.wait_recv()
+        for q in (free_up, free_dn, near_up, near_dn):
+            q.wait_recv()
         sfull[it, me_g] = (own + rbuf[it, 0].astype(F32) + rbuf[it, 1].astype(F32)).astype(BF16)
-        sent.extend([far_up, far_dn, near_up, near_dn])
-
-        def block(g, part=None):
-            return sfull.at[it, g] if part is None else sfull.at[it, g, part]
-
-        def send(n, g, part, peer):
-            out = copy(block(g, part), block(g, part), ag_ss.at[it, n], ag_rs.at[it, n], *peer)
+
+        def block(g, first, n):
+            return sfull.at[it, g, pl.ds(first * quarter, n * quarter)]
+
+        def send(n, g, first, count, peer):
+            out = copy(block(g, first, count), block(g, first, count), ag_ss.at[it, n], ag_rs.at[it, n], *peer)
             out.start()
             sent.append(out)
 
-        def arrive(n, g, part):
-            copy(block(g, part), block(g, part), ag_ss.at[it, n], ag_rs.at[it, n], *other).wait_recv()
+        def arrive(n, g, first, count):
+            copy(
+                block(g, first, count), block(g, first, count), ag_ss.at[it, n], ag_rs.at[it, n], *other
+            ).wait_recv()
 
         mine = me_g
         up_k, dn_k, far_k = (y * NK + mk for y in (y_up, y_dn, y_far))
@@ -354,86 +365,101 @@
 
         def gather(first, g):
             base = pl.multiple_of(g * shard, TILE)
-            s = sfull[it, g]
-            t = inner_contract(res[:, pl.ds(base, shard)], s)
-            u = inner_contract(s, s)
-            if first:
-                tacc[it] = t
-                gacc[it] = u
-            else:
-                tacc[it] = tacc[it] + t
-                gacc[it] = gacc[it] + u
-
-        send(0, mine, top, up)
-        send(1, mine, bot, dn)
-        send(2, mine, bot, up)
-        send(3, mine, top, dn)
-        send(4, mine, None, other)
+            t = inner_contract(res[:, pl.ds(base, shard)], sfull[it, g])
+            tacc[...] = t if first else tacc[...] + t
+
+        send(0, mine, 0, 1, up)
+        send(3, mine, 2, 1, dn)
+        send(1, mine, 1, 1, up)
+        send(4, mine, 3, 1, dn)
+        s = sfull[it, mine]
+        gram = inner_contract(s, s)
+        for i in range(ng):
+            gsrc[it, i] = gram[i * gr : (i + 1) * gr, :]
+        grow[it, me_g] = gsrc[it, me_g]
+        got_gr = spread(ng, me_g, g_peer, lambda to: gsrc.at[it, to], grow.at[it], gr_ss.at[it], gr_rs.at[it])
+        send(6, mine, 0, 4, other)
+        send(2, mine, 2, 2, up)
+        send(5, mine, 0, 2, dn)
         gather(True, mine)
-        arrive(0, dn_k, top)
-        send(5, dn_k, top, up)
-        arrive(1, up_k, bot)
-        send(6, up_k, bot, dn)
-        arrive(4, mine_o, None)
+        arrive(0, dn_k, 0, 1)
+        send(7, dn_k, 0, 1, up)
+        arrive(3, up_k, 2, 1)
+        send(9, up_k, 2, 1, dn)
+        arrive(1, dn_k, 1, 1)
+        send(8, dn_k, 1, 1, up)
+        arrive(4, up_k, 3, 1)
+        send(10, up_k, 3, 1, dn)
+        wait_all(got_gr)
+        gx[it, mx] = total([grow[it, i] for i in range(ng)], ng)
+        got_gx = spread(nx, mx, x_peer, lambda to: gx.at[it, mx], gx.at[it], gx_ss.at[it], gx_rs.at[it])
+        arrive(6, mine_o, 0, 4)
         gather(False, mine_o)
-        arrive(2, dn_k, bot)
-        send(7, dn_k, None, other)
-        arrive(3, up_k, top)
-        send(8, up_k, None, other)
+        arrive(2, dn_k, 2, 2)
+        send(11, dn_k, 0, 4, other)
+        arrive(5, up_k, 0, 2)
+        send(12, up_k, 0, 4, other)
         gather(False, dn_k)
         gather(False, up_k)
-        arrive(7, dn_o, None)
-        gather(False, dn_o)
-        arrive(8, up_o, None)
-        gather(False, up_o)
-        arrive(5, far_k, top)
-        arrive(6, far_k, bot)
-        send(9, far_k, None, other)
-        gather(False, far_k)
-        arrive(9, far_o, None)
-        gather(False, far_o)
-        if it == ITERS - 1:
-            leave = pltpu.make_async_copy(sfull.at[it], s_out, out_sem)
-            leave.start()
-
-        for i in range(nx):
-            txs[it, i] = tacc[it, pl.ds(i * blk, blk), :]
-        txr[it, mx] = txs[it, mx]
-        gx[it, mx] = gacc[it, pl.ds(pl.multiple_of(me_g * gr, 8), gr), :]
-        got_gx = spread(nx, mx, x_peer, lambda to: gx.at[it, mx], gx.at[it], gx_ss.at[it], gx_rs.at[it])
-        got_tx = spread(nx, mx, x_peer, lambda to: txs.at[it, to], txr.at[it], tx_ss.at[it], tx_rs.at[it])
         wait_all(got_gx)
         gz[it, mz] = total([gx[it, i] for i in range(nx)], nx)
         got_gz = spread(nz, mz, z_peer, lambda to: gz.at[it, mz], gz.at[it], gz_ss.at[it], gz_rs.at[it])
+        arrive(11, dn_o, 0, 4)
+        gather(False, dn_o)
+        arrive(7, far_k, 0, 1)
+        arrive(8, far_k, 1, 1)
+        send(13, far_k, 0, 2, other)
+        arrive(9, far_k, 2, 1)
+        arrive(10, far_k, 3, 1)
+        send(14, far_k, 2, 2, other)
+        arrive(12, up_o, 0, 4)
+        gather(False, up_o)
+        gather(False, far_k)
+        arrive(13, far_o, 0, 2)
+        arrive(14, far_o, 2, 2)
+        gather(False, far_o)
+
+        for i in range(nx):
+            txs[it, i] = tacc[pl.ds(i * blk, blk), :].astype(BF16)
+        txr[it, mx] = txs[it, mx]
+        got_tx = spread(nx, mx, x_peer, lambda to: txs.at[it, to], txr.at[it], tx_ss.at[it], tx_rs.at[it])
+        wait_all(got_gz)
+        gg[it, me_g] = total([gz[it, i] for i in range(nz)], nz)
+        got_gg = spread(ng, me_g, g_peer, lambda to: gg.at[it, me_g], gg.at[it], gg_ss.at[it], gg_rs.at[it])
         wait_all(got_tx)
-        tsum = total([txr[it, i] for i in range(nx)], nx)
+        tsum = total([txr[it, i].astype(F32) for i in range(nx)], nx).astype(BF16)
         for i in range(nz):
             tzs[it, i] = tsum[i * zr : (i + 1) * zr, :]
         tzr[it, mz] = tzs[it, mz]
         got_tz = spread(nz, mz, z_peer, lambda to: tzs.at[it, to], tzr.at[it], tz_ss.at[it], tz_rs.at[it])
-        wait_all(got_gz)
-        gg[it, me_g] = total([gz[it, i] for i in range(nz)], nz)
-        got_gg = spread(ng, me_g, g_peer, lambda to: gg.at[it, me_g], gg.at[it], gg_ss.at[it], gg_rs.at[it])
-        wait_all(got_tz)
-        tall[it, mx, mz] = total([tzr[it, i] for i in range(nz)], nz)
-        got_taz = spread(
-            nz, mz, z_peer, lambda to: tall.at[it, mx, mz], tall.at[it, mx], taz_ss.at[it], taz_rs.at[it]
-        )
-        wait_all(got_taz)
-        got_tax = spread(
-            nx, mx, x_peer, lambda to: tall.at[it, mx], tall.at[it], tax_ss.at[it], tax_rs.at[it]
-        )
         wait_all(got_gg)
         white = whiten(it)
+        wait_all(got_tz)
+        own = inner_contract(total([tzr[it, i].astype(F32) for i in range(nz)], nz), white, HIGHEST)
+        oall[it, mx, mz] = (own * gene_scale).astype(BF16)
+        got_oz = spread(
+            nz, mz, z_peer, lambda to: oall.at[it, mx, mz], oall.at[it, mx], taz_ss.at[it], taz_rs.at[it]
+        )
         if it == ITERS - 1:
-            w_out[...] = white
-        wait_all(got_tax)
+            up_front = jnp.transpose(white)
+            high = up_front.astype(BF16)
+            w_out[:, pl.ds(0, rank)] = high
+            w_out[:, pl.ds(rank, rank)] = (up_front - high.astype(F32)).astype(BF16)
+            for i in range(ng):
+                flat[i] = jnp.transpose(sfull[it, i])
+            leave = pltpu.make_async_copy(flat, s_out, out_sem)
+            leave.start()
+        wait_all(got_oz)
+        got_ox = spread(
+            nx, mx, x_peer, lambda to: oall.at[it, mx], oall.at[it], tax_ss.at[it], tax_rs.at[it]
+        )
+        wait_all(got_ox)
         for i in range(nx):
-            t = jnp.concatenate([tall[it, i, j] for j in range(nz)], axis=0)
+            loading = jnp.concatenate([oall[it, i, j] for j in range(nz)], axis=0)
             if it == ITERS - 1:
-                load_out[pl.ds(i * blk, blk), :] = inner_contract(t, white, HIGHEST) * gene_scale
+                load_out[pl.ds(i * blk, blk), :] = loading
             else:
-                omega[:, pl.ds(i * blk, blk)] = (inner_contract(white, t, HIGHEST) * gene_scale).astype(BF16)
+                omega[:, pl.ds(i * blk, blk)] = jnp.transpose(loading)
 
     leave.wait()
     for s in sent:
@@ -445,10 +471,10 @@
 
 
 def finish(s_ref, white_ref, load_ref, basis_ref, out_ref):
-    basis_ref[...] = lax.dot_general(
-        s_ref[0].astype(F32), white_ref[...], (((0,), (1,)), ((), ())), precision=HIGHEST, preferred_element_type=F32
-    )
-    out_ref[...] = load_ref[pl.ds(0, out_ref.shape[0]), :]
+    parts = jnp.dot(s_ref[...], white_ref[...], preferred_element_type=F32)
+    rank = parts.shape[1] // 2
+    basis_ref[...] = parts[:, :rank] + parts[:, rank:]
+    out_ref[...] = load_ref[pl.ds(0, out_ref.shape[0]), :].astype(F32)
 
 
 def shards(counts, sketch):
@@ -471,9 +497,9 @@
     s_all, white, load = pl.pallas_call(
         functools.partial(kernel, dims),
         out_shape=(
-            jax.ShapeDtypeStruct((ng, rank, shard), BF16),
-            jax.ShapeDtypeStruct((rank, rank), F32),
-            jax.ShapeDtypeStruct((wide, rank), F32),
+            jax.ShapeDtypeStruct((ng, shard, rank), BF16),
+            jax.ShapeDtypeStruct((rank, 2 * rank), BF16),
+            jax.ShapeDtypeStruct((wide, rank), BF16),
         ),
         in_specs=[pl.BlockSpec(memory_space=pl.ANY), pl.BlockSpec(memory_space=pltpu.VMEM)],
         out_specs=(
@@ -498,14 +524,17 @@
             V((ITERS, 3, rank, shard), BF16),
             V((ITERS, 2, rank // 2, shard), BF16),
             V((ITERS, 2, rank, shard), BF16),
+            V((2, rank // 2, shard), F32),
             V((ITERS, ng, rank, shard), BF16),
-            V((ITERS, wide, rank), F32),
-            V((ITERS, rank, rank), F32),
-            V((ITERS, nx, blk, rank), F32),
-            V((ITERS, nx, blk, rank), F32),
-            V((ITERS, nz, zr, rank), F32),
-            V((ITERS, nz, zr, rank), F32),
-            V((ITERS, nx, nz, zr, rank), F32),
+            V((ng, shard, rank), BF16),
+            V((wide, rank), F32),
+            V((ITERS, ng, gr, rank), F32),
+            V((ITERS, ng, gr, rank), F32),
+            V((ITERS, nx, blk, rank), BF16),
+            V((ITERS, nx, blk, rank), BF16),
+            V((ITERS, nz, zr, rank), BF16),
+            V((ITERS, nz, zr, rank), BF16),
+            V((ITERS, nx, nz, zr, rank), BF16),
             V((ITERS, nx, gr, rank), F32),
             V((ITERS, nz, gr, rank), F32),
             V((ITERS, ng, gr, rank), F32),
@@ -518,13 +547,13 @@
             *pairs(ng),
             *pairs(ng),
             *pairs(ITERS, 4),
-            *pairs(ITERS, 2),
-            *pairs(ITERS, 2),
-            *pairs(ITERS, 10),
+            *pairs(ITERS, 6),
+            *pairs(ITERS, 15),
             *pairs(ITERS, nx),
             *pairs(ITERS, nz),
             *pairs(ITERS, nz),
             *pairs(ITERS, nx),
+            *pairs(ITERS, ng),
             *pairs(ITERS, nx),
             *pairs(ITERS, nz),
             *pairs(ITERS, ng),
@@ -534,24 +563,25 @@
         ),
         name="sweep",
     )(counts.T, sketch)
+    step = rows // BLOCKS
     return pl.pallas_call(
         finish,
-        grid=(-(-rows // shard),),
+        grid=(BLOCKS,),
         out_shape=(
             jax.ShapeDtypeStruct((rows, rank), F32),
             jax.ShapeDtypeStruct((genes, rank), F32),
         ),
         in_specs=[
-            pl.BlockSpec((1, rank, shard), lambda i: (i, 0, 0)),
-            pl.BlockSpec((rank, rank), lambda i: (0, 0)),
+            pl.BlockSpec((step, rank), lambda i: (i, 0)),
+            pl.BlockSpec((rank, 2 * rank), lambda i: (0, 0)),
             pl.BlockSpec((wide, rank), lambda i: (0, 0)),
         ],
         out_specs=(
-            pl.BlockSpec((shard, rank), lambda i: (i, 0)),
+            pl.BlockSpec((step, rank), lambda i: (i, 0)),
             pl.BlockSpec((genes, rank), lambda i: (0, 0)),
         ),
         name="finish",
-    )(s_all, white, load)
+    )(s_all.reshape(ng * shard, rank), white, load)
 
 
 def solution(mesh):

time: 127 us -> 123 us (0.969)
  Pallas kernels: 126 us -> 121 us
    pallas_call x1, Pallas kernels: 7.56 us -> 4.32 us  [shards(): pl.pallas_call(finish, grid=(BLOCKS,), out_shape=(jax.ShapeDtypeStruct((r...]
    pallas_call x1, Pallas kernels: 118 us -> 117 us  [shards(): pl.pallas_call(functools.partial(kernel, dims), out_shape=(jax.ShapeDtype...]
where the time goes in v3:
time: 123 us; the launch traced here: 122 us
  Pallas kernels  121 us (98%)
    pallas_call x1, Pallas kernels, shards(): pl.pallas_call(functools.partial(kernel, dims), out_shape=(jax.ShapeDtype...  117 us
    pallas_call x1, Pallas kernels, shards(): pl.pallas_call(finish, grid=(BLOCKS,), out_shape=(jax.ShapeDtypeStruct((r...  4.32 us

profile of v3, /device:TPU:32, one launch (start us, length us, event | category | flops | bytes accessed | tf_op | source)
XLA Modules:
  0.0 121.6 jit_solution(4194796950097077690)
XLA Ops:
  0.6 116.6 %sweep.1 = (bf16[8,640,128]{2,1,0:T(8,128)(2,1)}, bf16[128,256]{1,0:T(8,128)(2,1)}, bf16[512,128]{1,0:T(8,128)(2,1)}) custom-call(s32[500,4864]{1,0:T(8,128)} %bitcast.2, bf16[500,128]{1,0:T(8,128)(2,1)} %sketch_ref.1), custom_call_target="tpu_custom_call" | custom-call | tf_op jit(solution)/shard_map/sweep/pallas_call | solution.py:497
  117.3 4.3 %finish.1 = (f32[4864,128]{1,0:T(8,128)}, f32[500,128]{1,0:T(8,128)}) custom-call(bf16[5120,128]{1,0:T(8,128)(2,1)} %bitcast.3, bf16[128,256]{1,0:T(8,128)(2,1)} %get-tuple-element.6.white_ref, bf16[512,128]{1,0:T(8,128)(2,1)} %get-tuple-element.7.load_ref), custom_call_target="tpu_custom_call" | custom-call | tf_op jit(solution)/shard_map/finish/pallas_call | solution.py:567

commit v4 on v3

--- a/solution.py
+++ b/solution.py
@@ -63,11 +63,15 @@
     tacc,
     gsrc,
     grow,
-    txs,
-    txr,
+    short_s,
+    short_r,
+    short_all,
+    wide_s,
+    wide_r,
+    wide_all,
     tzs,
     tzr,
-    oall,
+    halves,
     gx,
     gz,
     gg,
@@ -249,8 +253,9 @@
         lax.fori_loop(first, jnp.minimum(first + shard // TILE, rows // TILE), some, 0)
 
     gene_scale = math.sqrt(n_genes) / n_cells
-
-    def whiten(it):
+    shorts, wides = (short_s, short_r, short_all), (wide_s, wide_r, wide_all)
+
+    def shift_gram(it):
         eye = (
             lax.broadcasted_iota(jnp.int32, (rank, rank), 0)
             == lax.broadcasted_iota(jnp.int32, (rank, rank), 1)
@@ -259,6 +264,8 @@
         diagonal = jnp.sum(jnp.sum(jnp.where(eye, gram, 0.0), axis=1, keepdims=True), axis=0, keepdims=True)
         aug[:, pl.ds(0, rank)] = gram + jnp.where(eye, 1e-05 * diagonal / rank, 0.0)
         aug[:, pl.ds(rank, rank)] = jnp.where(eye, 1.0, 0.0)
+
+    def panels(first, last):
         lane = lax.broadcasted_iota(jnp.int32, (PANEL, rank), 1)
         row = lax.broadcasted_iota(jnp.int32, (PANEL, 2 * rank), 0)
 
@@ -280,8 +287,7 @@
             aug[...] = aug[...] - outer_contract(lines[:, :rank], lines, HIGHEST)
             return carry
 
-        lax.fori_loop(0, rank // PANEL, panel, 0)
-        return linv[...] * math.sqrt(n_cells)
+        lax.fori_loop(first, last, panel, 0)
 
     for it in range(ITERS):
         order = (y_far, y_up, y_dn, my)
@@ -419,47 +425,56 @@
         arrive(14, far_o, 2, 2)
         gather(False, far_o)
 
+        txs, txr, tall = wides if it == ITERS - 1 else shorts
         for i in range(nx):
-            txs[it, i] = tacc[pl.ds(i * blk, blk), :].astype(BF16)
-        txr[it, mx] = txs[it, mx]
-        got_tx = spread(nx, mx, x_peer, lambda to: txs.at[it, to], txr.at[it], tx_ss.at[it], tx_rs.at[it])
+            txs[i] = tacc[pl.ds(i * blk, blk), :].astype(txs.dtype)
+        txr[mx] = txs[mx]
+        got_tx = spread(nx, mx, x_peer, lambda to: txs.at[to], txr, tx_ss.at[it], tx_rs.at[it])
         wait_all(got_gz)
         gg[it, me_g] = total([gz[it, i] for i in range(nz)], nz)
         got_gg = spread(ng, me_g, g_peer, lambda to: gg.at[it, me_g], gg.at[it], gg_ss.at[it], gg_rs.at[it])
         wait_all(got_tx)
-        tsum = total([txr[it, i].astype(F32) for i in range(nx)], nx).astype(BF16)
+        tsum = total([txr[i].astype(F32) for i in range(nx)], nx)
         for i in range(nz):
             tzs[it, i] = tsum[i * zr : (i + 1) * zr, :]
         tzr[it, mz] = tzs[it, mz]
         got_tz = spread(nz, mz, z_peer, lambda to: tzs.at[it, to], tzr.at[it], tz_ss.at[it], tz_rs.at[it])
-        wait_all(got_gg)
-        white = whiten(it)
-        wait_all(got_tz)
-        own = inner_contract(total([tzr[it, i].astype(F32) for i in range(nz)], nz), white, HIGHEST)
-        oall[it, mx, mz] = (own * gene_scale).astype(BF16)
-        got_oz = spread(
-            nz, mz, z_peer, lambda to: oall.at[it, mx, mz], oall.at[it, mx], taz_ss.at[it], taz_rs.at[it]
-        )
         if it == ITERS - 1:
-            up_front = jnp.transpose(white)
-            high = up_front.astype(BF16)
-            w_out[:, pl.ds(0, rank)] = high
-            w_out[:, pl.ds(rank, rank)] = (up_front - high.astype(F32)).astype(BF16)
             for i in range(ng):
                 flat[i] = jnp.transpose(sfull[it, i])
             leave = pltpu.make_async_copy(flat, s_out, out_sem)
             leave.start()
-        wait_all(got_oz)
-        got_ox = spread(
-            nx, mx, x_peer, lambda to: oall.at[it, mx], oall.at[it], tax_ss.at[it], tax_rs.at[it]
+        wait_all(got_tz)
+        tall[mx, mz] = total([tzr[it, i] for i in range(nz)], nz).astype(tall.dtype)
+        got_taz = spread(
+            nz, mz, z_peer, lambda to: tall.at[mx, mz], tall.at[mx], taz_ss.at[it], taz_rs.at[it]
         )
-        wait_all(got_ox)
+        wait_all(got_gg)
+        shift_gram(it)
+        panels(0, rank // PANEL * 5 // 8)
+        wait_all(got_taz)
+        got_tax = spread(
+            nx, mx, x_peer, lambda to: tall.at[mx], tall, tax_ss.at[it], tax_rs.at[it]
+        )
+        panels(rank // PANEL * 5 // 8, rank // PANEL)
+        white = linv[...] * math.sqrt(n_cells)
+        front = jnp.transpose(white) if it == ITERS - 1 else white
+        high = front.astype(BF16)
+        low = (front - high.astype(F32)).astype(BF16)
+        if it == ITERS - 1:
+            w_out[:, pl.ds(0, rank)] = high
+            w_out[:, pl.ds(rank, rank)] = low
+        else:
+            halves[pl.ds(0, rank), :] = high
+            halves[pl.ds(rank, rank), :] = low
+        wait_all(got_tax)
         for i in range(nx):
-            loading = jnp.concatenate([oall[it, i, j] for j in range(nz)], axis=0)
+            t = jnp.concatenate([tall[i, j] for j in range(nz)], axis=0)
             if it == ITERS - 1:
-                load_out[pl.ds(i * blk, blk), :] = loading
+                load_out[pl.ds(i * blk, blk), :] = inner_contract(t, white, HIGHEST) * gene_scale
             else:
-                omega[:, pl.ds(i * blk, blk)] = jnp.transpose(loading)
+                flip = inner_contract(halves[...], t)
+                omega[:, pl.ds(i * blk, blk)] = ((flip[:rank] + flip[rank:]) * gene_scale).astype(BF16)
 
     leave.wait()
     for s in sent:
@@ -474,7 +489,7 @@
     parts = jnp.dot(s_ref[...], white_ref[...], preferred_element_type=F32)
     rank = parts.shape[1] // 2
     basis_ref[...] = parts[:, :rank] + parts[:, rank:]
-    out_ref[...] = load_ref[pl.ds(0, out_ref.shape[0]), :].astype(F32)
+    out_ref[...] = load_ref[pl.ds(0, out_ref.shape[0]), :]
 
 
 def shards(counts, sketch):
@@ -499,7 +514,7 @@
         out_shape=(
             jax.ShapeDtypeStruct((ng, shard, rank), BF16),
             jax.ShapeDtypeStruct((rank, 2 * rank), BF16),
-            jax.ShapeDtypeStruct((wide, rank), BF16),
+            jax.ShapeDtypeStruct((wide, rank), F32),
         ),
         in_specs=[pl.BlockSpec(memory_space=pl.ANY), pl.BlockSpec(memory_space=pltpu.VMEM)],
         out_specs=(
@@ -530,11 +545,15 @@
             V((wide, rank), F32),
             V((ITERS, ng, gr, rank), F32),
             V((ITERS, ng, gr, rank), F32),
-            V((ITERS, nx, blk, rank), BF16),
-            V((ITERS, nx, blk, rank), BF16),
-            V((ITERS, nz, zr, rank), BF16),
-            V((ITERS, nz, zr, rank), BF16),
-            V((ITERS, nx, nz, zr, rank), BF16),
+            V((nx, blk, rank), BF16),
+            V((nx, blk, rank), BF16),
+            V((nx, nz, zr, rank), BF16),
+            V((nx, blk, rank), F32),
+            V((nx, blk, rank), F32),
+            V((nx, nz, zr, rank), F32),
+            V((ITERS, nz, zr, rank), F32),
+            V((ITERS, nz, zr, rank), F32),
+            V((2 * rank, rank), BF16),
             V((ITERS, nx, gr, rank), F32),
             V((ITERS, nz, gr, rank), F32),
             V((ITERS, ng, gr, rank), F32),

time: 123 us -> 115 us (0.935)
  Pallas kernels: 121 us -> 114 us
    pallas_call x1, Pallas kernels: 117 us -> 109 us  [shards(): pl.pallas_call(functools.partial(kernel, dims), out_shape=(jax.ShapeDtype...]
where the time goes in v4:
time: 115 us; the launch traced here: 114 us
  Pallas kernels  114 us (99%)
    pallas_call x1, Pallas kernels, shards(): pl.pallas_call(functools.partial(kernel, dims), out_shape=(jax.ShapeDtype...  109 us
    pallas_call x1, Pallas kernels, shards(): pl.pallas_call(finish, grid=(BLOCKS,), out_shape=(jax.ShapeDtypeStruct((r...  4.38 us

profile of v4, /device:TPU:32, one launch (start us, length us, event | category | flops | bytes accessed | tf_op | source)
XLA Modules:
  0.0 114.3 jit_solution(11031287149645171438)
XLA Ops:
  0.6 109.3 %sweep.1 = (bf16[8,640,128]{2,1,0:T(8,128)(2,1)}, bf16[128,256]{1,0:T(8,128)(2,1)}, f32[512,128]{1,0:T(8,128)}) custom-call(s32[500,4864]{1,0:T(8,128)} %bitcast.2, bf16[500,128]{1,0:T(8,128)(2,1)} %sketch_ref.1), custom_call_target="tpu_custom_call" | custom-call | tf_op jit(solution)/shard_map/sweep/pallas_call | solution.py:512
  109.9 4.4 %finish.1 = (f32[4864,128]{1,0:T(8,128)}, f32[500,128]{1,0:T(8,128)}) custom-call(bf16[5120,128]{1,0:T(8,128)(2,1)} %bitcast.3, bf16[128,256]{1,0:T(8,128)(2,1)} %get-tuple-element.6.white_ref, f32[512,128]{1,0:T(8,128)} %get-tuple-element.7.load_ref), custom_call_target="tpu_custom_call" | custom-call | tf_op jit(solution)/shard_map/finish/pallas_call | solution.py:586

commit v5 on v4

--- a/solution.py
+++ b/solution.py
@@ -15,7 +15,7 @@
 STEP = 32
 PANEL = 8
 PER = 2
-BLOCKS = 4
+BLOCKS = 2
 HIGHEST = lax.Precision.HIGHEST
 MESH = pl.DeviceIdType.MESH
 F32 = jnp.float32
@@ -46,8 +46,7 @@
     gpart,
     cellx,
     totc,
-    genex,
-    genez,
+    genec,
     grp,
     fracs,
     omega,
@@ -81,8 +80,6 @@
     out_sem,
     bx_ss,
     bx_rs,
-    bz_ss,
-    bz_rs,
     ba_ss,
     ba_rs,
     bg_ss,
@@ -93,6 +90,10 @@
     f_rs,
     ag_ss,
     ag_rs,
+    dr_ss,
+    dr_rs,
+    da_ss,
+    da_rs,
     tx_ss,
     tx_rs,
     tz_ss,
@@ -112,6 +113,7 @@
 ):
     nx, nz, ng, rows, genes, wide, rank, n_cells, n_genes = dims
     ny = ng // NK
+    nc = nx * nz
     shard = shard_of(rows, ng)
     half, quarter = rank // 2, rank // 4
     blk = wide // nx
@@ -129,6 +131,9 @@
             src_ref=src, dst_ref=dst, send_sem=ss, recv_sem=rs, device_id=(c, g), device_id_type=MESH
         )
 
+    def c_peer(i):
+        return i, me_g
+
     def x_peer(i):
         return mz * nx + i, me_g
 
@@ -161,7 +166,7 @@
         return acc
 
     barrier = pltpu.get_barrier_semaphore()
-    for n, me, peer in ((nx, mx, x_peer), (nz, mz, z_peer), (ng, me_g, g_peer)):
+    for n, me, peer in ((nc, me_c, c_peer), (ng, me_g, g_peer)):
         for d in range(1, n):
             pl.semaphore_signal(barrier, inc=1, device_id=peer(lax.rem(me + d, n)), device_id_type=MESH)
 
@@ -203,18 +208,15 @@
         line = gpart[pl.ds(g * TILE, n), :].astype(F32)
         if n < TILE:
             line = jnp.concatenate([line, jnp.zeros((TILE - n, TILE), F32)], axis=0)
-        genex[mx, :, pl.ds(g * TILE, TILE)] = jnp.sum(jnp.transpose(line), axis=0, keepdims=True)
-
-    pl.semaphore_wait(barrier, nx + nz + ng - 3)
-    got_x = spread(nx, mx, x_peer, lambda to: genex.at[mx], genex, bx_ss, bx_rs)
+        genec[me_c, :, pl.ds(g * TILE, TILE)] = jnp.sum(jnp.transpose(line), axis=0, keepdims=True)
+
+    pl.semaphore_wait(barrier, nc + ng - 2)
+    got_c = spread(nc, me_c, c_peer, lambda to: genec.at[me_c], genec, bx_ss, bx_rs)
     got_a = spread(ng, me_g, g_peer, lambda to: cellx.at[me_g], cellx, ba_ss, ba_rs)
-    wait_all(got_x)
-    genez[mz] = total(genex, nx)
-    got_z = spread(nz, mz, z_peer, lambda to: genez.at[mz], genez, bz_ss, bz_rs)
     wait_all(got_a)
     totc[...] = total(cellx, ng)
-    wait_all(got_z)
-    gene_total = total(genez, nz)
+    wait_all(got_c)
+    gene_total = total(genec, nc)
     short = gene_total[:, :TILE]
     for g in range(1, groups):
         short = short + gene_total[:, g * TILE : (g + 1) * TILE]
@@ -253,7 +255,7 @@
         lax.fori_loop(first, jnp.minimum(first + shard // TILE, rows // TILE), some, 0)
 
     gene_scale = math.sqrt(n_genes) / n_cells
-    shorts, wides = (short_s, short_r, short_all), (wide_s, wide_r, wide_all)
+    piece = wide // nc
 
     def shift_gram(it):
         eye = (
@@ -396,20 +398,17 @@
         send(8, dn_k, 1, 1, up)
         arrive(4, up_k, 3, 1)
         send(10, up_k, 3, 1, dn)
+        arrive(6, mine_o, 0, 4)
+        gather(False, mine_o)
         wait_all(got_gr)
         gx[it, mx] = total([grow[it, i] for i in range(ng)], ng)
         got_gx = spread(nx, mx, x_peer, lambda to: gx.at[it, mx], gx.at[it], gx_ss.at[it], gx_rs.at[it])
-        arrive(6, mine_o, 0, 4)
-        gather(False, mine_o)
         arrive(2, dn_k, 2, 2)
         send(11, dn_k, 0, 4, other)
         arrive(5, up_k, 0, 2)
         send(12, up_k, 0, 4, other)
         gather(False, dn_k)
         gather(False, up_k)
-        wait_all(got_gx)
-        gz[it, mz] = total([gx[it, i] for i in range(nx)], nx)
-        got_gz = spread(nz, mz, z_peer, lambda to: gz.at[it, mz], gz.at[it], gz_ss.at[it], gz_rs.at[it])
         arrive(11, dn_o, 0, 4)
         gather(False, dn_o)
         arrive(7, far_k, 0, 1)
@@ -418,6 +417,9 @@
         arrive(9, far_k, 2, 1)
         arrive(10, far_k, 3, 1)
         send(14, far_k, 2, 2, other)
+        wait_all(got_gx)
+        gz[it, mz] = total([gx[it, i] for i in range(nx)], nx)
+        got_gz = spread(nz, mz, z_peer, lambda to: gz.at[it, mz], gz.at[it], gz_ss.at[it], gz_rs.at[it])
         arrive(12, up_o, 0, 4)
         gather(False, up_o)
         gather(False, far_k)
@@ -425,37 +427,46 @@
         arrive(14, far_o, 2, 2)
         gather(False, far_o)
 
-        txs, txr, tall = wides if it == ITERS - 1 else shorts
-        for i in range(nx):
-            txs[i] = tacc[pl.ds(i * blk, blk), :].astype(txs.dtype)
-        txr[mx] = txs[mx]
-        got_tx = spread(nx, mx, x_peer, lambda to: txs.at[to], txr, tx_ss.at[it], tx_rs.at[it])
+        straight = it < ITERS - 1
+        if straight:
+            for i in range(nc):
+                short_s[i] = tacc[pl.ds(i * piece, piece), :].astype(BF16)
+            short_r[me_c] = short_s[me_c]
+            got_tx = spread(nc, me_c, c_peer, lambda to: short_s.at[to], short_r, dr_ss, dr_rs)
+        else:
+            for i in range(nx):
+                wide_s[i] = tacc[pl.ds(i * blk, blk), :]
+            wide_r[mx] = wide_s[mx]
+            got_tx = spread(nx, mx, x_peer, lambda to: wide_s.at[to], wide_r, tx_ss, tx_rs)
         wait_all(got_gz)
         gg[it, me_g] = total([gz[it, i] for i in range(nz)], nz)
         got_gg = spread(ng, me_g, g_peer, lambda to: gg.at[it, me_g], gg.at[it], gg_ss.at[it], gg_rs.at[it])
         wait_all(got_tx)
-        tsum = total([txr[i].astype(F32) for i in range(nx)], nx)
-        for i in range(nz):
-            tzs[it, i] = tsum[i * zr : (i + 1) * zr, :]
-        tzr[it, mz] = tzs[it, mz]
-        got_tz = spread(nz, mz, z_peer, lambda to: tzs.at[it, to], tzr.at[it], tz_ss.at[it], tz_rs.at[it])
+        if straight:
+            tsum = total([short_r[i].astype(F32) for i in range(nc)], nc)
+            short_all[me_c] = tsum.astype(BF16)
+            got_all = spread(nc, me_c, c_peer, lambda to: short_all.at[me_c], short_all, da_ss, da_rs)
+        else:
+            tsum = total([wide_r[i] for i in range(nx)], nx)
+            for i in range(nz):
+                tzs[i] = tsum[i * zr : (i + 1) * zr, :]
+            tzr[mz] = tzs[mz]
+            got_tz = spread(nz, mz, z_peer, lambda to: tzs.at[to], tzr, tz_ss, tz_rs)
         if it == ITERS - 1:
             for i in range(ng):
                 flat[i] = jnp.transpose(sfull[it, i])
             leave = pltpu.make_async_copy(flat, s_out, out_sem)
             leave.start()
-        wait_all(got_tz)
-        tall[mx, mz] = total([tzr[it, i] for i in range(nz)], nz).astype(tall.dtype)
-        got_taz = spread(
-            nz, mz, z_peer, lambda to: tall.at[mx, mz], tall.at[mx], taz_ss.at[it], taz_rs.at[it]
-        )
+        if not straight:
+            wait_all(got_tz)
+            wide_all[mx, mz] = total([tzr[i] for i in range(nz)], nz)
+            got_taz = spread(nz, mz, z_peer, lambda to: wide_all.at[mx, mz], wide_all.at[mx], taz_ss, taz_rs)
         wait_all(got_gg)
         shift_gram(it)
         panels(0, rank // PANEL * 5 // 8)
-        wait_all(got_taz)
-        got_tax = spread(
-            nx, mx, x_peer, lambda to: tall.at[mx], tall, tax_ss.at[it], tax_rs.at[it]
-        )
+        if not straight:
+            wait_all(got_taz)
+            got_all = spread(nx, mx, x_peer, lambda to: wide_all.at[mx], wide_all, tax_ss, tax_rs)
         panels(rank // PANEL * 5 // 8, rank // PANEL)
         white = linv[...] * math.sqrt(n_cells)
         front = jnp.transpose(white) if it == ITERS - 1 else white
@@ -467,14 +478,16 @@
         else:
             halves[pl.ds(0, rank), :] = high
             halves[pl.ds(rank, rank), :] = low
-        wait_all(got_tax)
-        for i in range(nx):
-            t = jnp.concatenate([tall[i, j] for j in range(nz)], axis=0)
-            if it == ITERS - 1:
-                load_out[pl.ds(i * blk, blk), :] = inner_contract(t, white, HIGHEST) * gene_scale
-            else:
+        wait_all(got_all)
+        if straight:
+            for i in range(nx):
+                t = jnp.concatenate([short_all[i * nz + j] for j in range(nz)], axis=0)
                 flip = inner_contract(halves[...], t)
                 omega[:, pl.ds(i * blk, blk)] = ((flip[:rank] + flip[rank:]) * gene_scale).astype(BF16)
+        else:
+            for i in range(nx):
+                t = jnp.concatenate([wide_all[i, j] for j in range(nz)], axis=0)
+                load_out[pl.ds(i * blk, blk), :] = inner_contract(t, white, HIGHEST) * gene_scale
 
     leave.wait()
     for s in sent:
@@ -528,8 +541,7 @@
             V((genes, TILE), jnp.int32),
             V((ng, 1, rows), F32),
             V((1, rows), F32),
-            V((nx, 1, wide), F32),
-            V((nz, 1, wide), F32),
+            V((nc, 1, wide), F32),
             V((ng, 1, TILE), F32),
             V((wide, TILE), F32),
             V((rank, wide), BF16),
@@ -545,14 +557,14 @@
             V((wide, rank), F32),
             V((ITERS, ng, gr, rank), F32),
             V((ITERS, ng, gr, rank), F32),
-            V((nx, blk, rank), BF16),
-            V((nx, blk, rank), BF16),
-            V((nx, nz, zr, rank), BF16),
+            V((nc, wide // nc, rank), BF16),
+            V((nc, wide // nc, rank), BF16),
+            V((nc, wide // nc, rank), BF16),
             V((nx, blk, rank), F32),
             V((nx, blk, rank), F32),
             V((nx, nz, zr, rank), F32),
-            V((ITERS, nz, zr, rank), F32),
-            V((ITERS, nz, zr, rank), F32),
+            V((nz, zr, rank), F32),
+            V((nz, zr, rank), F32),
             V((2 * rank, rank), BF16),
             V((ITERS, nx, gr, rank), F32),
             V((ITERS, nz, gr, rank), F32),
@@ -561,17 +573,18 @@
             V((rank, rank), F32),
             D((rows // (PER * TILE),)),
             D,
-            *pairs(nx),
-            *pairs(nz),
+            *pairs(nc),
             *pairs(ng),
             *pairs(ng),
             *pairs(ITERS, 4),
             *pairs(ITERS, 6),
             *pairs(ITERS, 15),
-            *pairs(ITERS, nx),
-            *pairs(ITERS, nz),
-            *pairs(ITERS, nz),
-            *pairs(ITERS, nx),
+            *pairs(nc),
+            *pairs(nc),
+            *pairs(nx),
+            *pairs(nz),
+            *pairs(nz),
+            *pairs(nx),
             *pairs(ITERS, ng),
             *pairs(ITERS, nx),
             *pairs(ITERS, nz),

time: 115 us -> 109 us (0.948)
  Pallas kernels: 114 us -> 107 us
    pallas_call x1, Pallas kernels: 109 us -> 104 us  [shards(): pl.pallas_call(functools.partial(kernel, dims), out_shape=(jax.ShapeDtype...]
    pallas_call x1, Pallas kernels: 4.38 us -> 3.18 us  [shards(): pl.pallas_call(finish, grid=(BLOCKS,), out_shape=(jax.ShapeDtypeStruct((r...]
where the time goes in v5:
time: 109 us; the launch traced here: 108 us
  Pallas kernels  107 us (98%)
    pallas_call x1, Pallas kernels, shards(): pl.pallas_call(functools.partial(kernel, dims), out_shape=(jax.ShapeDtype...  104 us
    pallas_call x1, Pallas kernels, shards(): pl.pallas_call(finish, grid=(BLOCKS,), out_shape=(jax.ShapeDtypeStruct((r...  3.18 us

profile of v5, /device:TPU:32, one launch (start us, length us, event | category | flops | bytes accessed | tf_op | source)
XLA Modules:
  0.0 108.0 jit_solution(9293947717095170339)
XLA Ops:
  0.6 104.2 %sweep.1 = (bf16[8,640,128]{2,1,0:T(8,128)(2,1)}, bf16[128,256]{1,0:T(8,128)(2,1)}, f32[512,128]{1,0:T(8,128)}) custom-call(s32[500,4864]{1,0:T(8,128)} %bitcast.2, bf16[500,128]{1,0:T(8,128)(2,1)} %sketch_ref.1), custom_call_target="tpu_custom_call" | custom-call | tf_op jit(solution)/shard_map/sweep/pallas_call | solution.py:525
  104.8 3.2 %finish.1 = (f32[4864,128]{1,0:T(8,128)}, f32[500,128]{1,0:T(8,128)}) custom-call(bf16[5120,128]{1,0:T(8,128)(2,1)} %bitcast.3, bf16[128,256]{1,0:T(8,128)(2,1)} %get-tuple-element.6.white_ref, f32[512,128]{1,0:T(8,128)} %get-tuple-element.7.load_ref), custom_call_target="tpu_custom_call" | custom-call | tf_op jit(solution)/shard_map/finish/pallas_call | solution.py:599

commit v6 on v5

--- a/solution.py
+++ b/solution.py
@@ -37,7 +37,7 @@
 def kernel(
     dims,
     counts_hbm,
-    sketch_ref,
+    sketch_hbm,
     s_out,
     w_out,
     load_out,
@@ -76,7 +76,9 @@
     gg,
     aug,
     linv,
+    sketch,
     load_sem,
+    take_sem,
     out_sem,
     bx_ss,
     bx_rs,
@@ -165,24 +167,24 @@
             acc = acc + slots[i]
         return acc
 
+    per = PER * TILE
+    loads = rows // per
+
+    def load(i):
+        part = pl.ds(pl.multiple_of(i * per, TILE), per)
+        return pltpu.make_async_copy(counts_hbm.at[:, part], cnt.at[:, part], load_sem.at[i])
+
+    for i in range(loads):
+        load(i).start()
+    take = pltpu.make_async_copy(sketch_hbm, sketch, take_sem)
+    take.start()
+
     barrier = pltpu.get_barrier_semaphore()
     for n, me, peer in ((nc, me_c, c_peer), (ng, me_g, g_peer)):
         for d in range(1, n):
             pl.semaphore_signal(barrier, inc=1, device_id=peer(lax.rem(me + d, n)), device_id_type=MESH)
 
-    per = PER * TILE
-    loads = rows // per
-
-    def load(i):
-        part = pl.ds(pl.multiple_of(i * per, TILE), per)
-        return pltpu.make_async_copy(counts_hbm.at[:, part], cnt.at[:, part], load_sem.at[i])
-
-    for i in range(loads):
-        load(i).start()
-
     res[:, pl.ds(rows, ng * shard - rows)] = jnp.zeros((wide, ng * shard - rows), BF16)
-    flip = jnp.transpose(sketch_ref[...].astype(F32))
-    omega[...] = jnp.concatenate([flip, jnp.zeros((rank, wide - genes), F32)], axis=1).astype(BF16)
     gpart[...] = jnp.zeros((genes, TILE), jnp.int32)
     even = genes - genes % 8
 
@@ -213,6 +215,9 @@
     pl.semaphore_wait(barrier, nc + ng - 2)
     got_c = spread(nc, me_c, c_peer, lambda to: genec.at[me_c], genec, bx_ss, bx_rs)
     got_a = spread(ng, me_g, g_peer, lambda to: cellx.at[me_g], cellx, ba_ss, ba_rs)
+    take.wait()
+    flip = jnp.transpose(sketch[...].astype(F32))
+    omega[...] = jnp.concatenate([flip, jnp.zeros((rank, wide - genes), F32)], axis=1).astype(BF16)
     wait_all(got_a)
     totc[...] = total(cellx, ng)
     wait_all(got_c)
@@ -294,22 +299,21 @@
     for it in range(ITERS):
         order = (y_far, y_up, y_dn, my)
 
-        def pair(n):
-            for k in (ok, mk):
-                g = order[n] * NK + k
-                base = pl.multiple_of(g * shard, TILE)
-                if it == 0:
-                    residuals(g)
-                part = jnp.dot(omega[...], res[:, pl.ds(base, shard)], preferred_element_type=F32)
-                if k is ok:
-                    psend[it, n] = part
-                    out = copy(
-                        psend.at[it, n], precv.at[it, n], pr_ss.at[it, n], pr_rs.at[it, n], *g_peer(my * NK + ok)
-                    )
-                    out.start()
-                    sent.append(out)
-                else:
-                    pown[n] = part
+        def part(n, k):
+            g = order[n] * NK + k
+            base = pl.multiple_of(g * shard, TILE)
+            if it == 0:
+                residuals(g)
+            sums = jnp.dot(omega[...], res[:, pl.ds(base, shard)], preferred_element_type=F32)
+            if k is ok:
+                psend[it, n] = sums
+                out = copy(
+                    psend.at[it, n], precv.at[it, n], pr_ss.at[it, n], pr_rs.at[it, n], *g_peer(my * NK + ok)
+                )
+                out.start()
+                sent.append(out)
+            else:
+                pown[n] = sums
 
         def both(n):
             copy(
@@ -327,21 +331,28 @@
             sent.append(out)
             return out
 
-        pair(0)
-        pair(1)
+        part(0, ok)
+        part(0, mk)
+        part(1, ok)
+        if it > 0:
+            part(2, ok)
         qbuf[it, 0] = both(0).astype(BF16)
         far_up = hop(qbuf.at[it, 0, top], fbuf.at[it, 0], 0, up)
         far_dn = hop(qbuf.at[it, 0, bot], fbuf.at[it, 1], 1, dn)
+        if it == 0:
+            part(2, ok)
+        part(1, mk)
         q = both(1)
         qbuf[it, 1, bot] = q[half:].astype(BF16)
         late[0] = q[:half]
         free_up = hop(qbuf.at[it, 1, bot], rbuf.at[it, 0, bot], 2, up)
-        pair(2)
+        part(2, mk)
         q = both(2)
         qbuf[it, 2, top] = q[:half].astype(BF16)
         late[1] = q[half:]
         free_dn = hop(qbuf.at[it, 2, top], rbuf.at[it, 1, top], 3, dn)
-        pair(3)
+        part(3, ok)
+        part(3, mk)
         far_up.wait_recv()
         qbuf[it, 1, top] = (late[0] + fbuf[it, 0].astype(F32)).astype(BF16)
         near_up = hop(qbuf.at[it, 1, top], rbuf.at[it, 0, top], 4, up)
@@ -529,7 +540,7 @@
             jax.ShapeDtypeStruct((rank, 2 * rank), BF16),
             jax.ShapeDtypeStruct((wide, rank), F32),
         ),
-        in_specs=[pl.BlockSpec(memory_space=pl.ANY), pl.BlockSpec(memory_space=pltpu.VMEM)],
+        in_specs=[pl.BlockSpec(memory_space=pl.ANY), pl.BlockSpec(memory_space=pl.ANY)],
         out_specs=(
             pl.BlockSpec(memory_space=pl.ANY),
             pl.BlockSpec(memory_space=pltpu.VMEM),
@@ -571,7 +582,9 @@
             V((ITERS, ng, gr, rank), F32),
             V((rank, 2 * rank), F32),
             V((rank, rank), F32),
+            V((genes, rank), BF16),
             D((rows // (PER * TILE),)),
+            D,
             D,
             *pairs(nc),
             *pairs(ng),

time: 109 us -> 108 us (level)
    pallas_call x1, Pallas kernels: 104 us -> 103 us  [shards(): pl.pallas_call(functools.partial(kernel, dims), out_shape=(jax.ShapeDtype...]
where the time goes in v6:
time: 108 us; the launch traced here: 106 us
  Pallas kernels  106 us (98%)
    pallas_call x1, Pallas kernels, shards(): pl.pallas_call(functools.partial(kernel, dims), out_shape=(jax.ShapeDtype...  103 us
    pallas_call x1, Pallas kernels, shards(): pl.pallas_call(finish, grid=(BLOCKS,), out_shape=(jax.ShapeDtypeStruct((r...  3.18 us

profile of v6, /device:TPU:32, one launch (start us, length us, event | category | flops | bytes accessed | tf_op | source)
XLA Modules:
  0.0 106.3 jit_solution(18369381264105968292)
XLA Ops:
  0.6 102.5 %sweep.1 = (bf16[8,640,128]{2,1,0:T(8,128)(2,1)}, bf16[128,256]{1,0:T(8,128)(2,1)}, f32[512,128]{1,0:T(8,128)}) custom-call(s32[500,4864]{1,0:T(8,128)} %bitcast.2, bf16[500,128]{1,0:T(8,128)(2,1)} %sketch_hbm.1), custom_call_target="tpu_custom_call" | custom-call | tf_op jit(solution)/shard_map/sweep/pallas_call | solution.py:536
  103.2 3.2 %finish.1 = (f32[4864,128]{1,0:T(8,128)}, f32[500,128]{1,0:T(8,128)}) custom-call(bf16[5120,128]{1,0:T(8,128)(2,1)} %bitcast.3, bf16[128,256]{1,0:T(8,128)(2,1)} %get-tuple-element.6.white_ref, f32[512,128]{1,0:T(8,128)} %get-tuple-element.7.load_ref), custom_call_target="tpu_custom_call" | custom-call | tf_op jit(solution)/shard_map/finish/pallas_call | solution.py:612

commit v7 on v6

--- a/solution.py
+++ b/solution.py
@@ -67,7 +67,7 @@
     short_all,
     wide_s,
     wide_r,
-    wide_all,
+    last,
     tzs,
     tzr,
     halves,
@@ -100,10 +100,8 @@
     tx_rs,
     tz_ss,
     tz_rs,
-    taz_ss,
-    taz_rs,
-    tax_ss,
-    tax_rs,
+    la_ss,
+    la_rs,
     gr_ss,
     gr_rs,
     gx_ss,
@@ -463,23 +461,19 @@
                 tzs[i] = tsum[i * zr : (i + 1) * zr, :]
             tzr[mz] = tzs[mz]
             got_tz = spread(nz, mz, z_peer, lambda to: tzs.at[to], tzr, tz_ss, tz_rs)
-        if it == ITERS - 1:
+        wait_all(got_gg)
+        shift_gram(it)
+        panels(0, rank // PANEL)
+        white = linv[...] * math.sqrt(n_cells)
+        if not straight:
+            wait_all(got_tz)
+            own = inner_contract(total([tzr[i] for i in range(nz)], nz), white, HIGHEST)
+            last[me_c] = (own * gene_scale).astype(BF16)
+            got_all = spread(nc, me_c, c_peer, lambda to: last.at[me_c], last, la_ss, la_rs)
             for i in range(ng):
                 flat[i] = jnp.transpose(sfull[it, i])
             leave = pltpu.make_async_copy(flat, s_out, out_sem)
             leave.start()
-        if not straight:
-            wait_all(got_tz)
-            wide_all[mx, mz] = total([tzr[i] for i in range(nz)], nz)
-            got_taz = spread(nz, mz, z_peer, lambda to: wide_all.at[mx, mz], wide_all.at[mx], taz_ss, taz_rs)
-        wait_all(got_gg)
-        shift_gram(it)
-        panels(0, rank // PANEL * 5 // 8)
-        if not straight:
-            wait_all(got_taz)
-            got_all = spread(nx, mx, x_peer, lambda to: wide_all.at[mx], wide_all, tax_ss, tax_rs)
-        panels(rank // PANEL * 5 // 8, rank // PANEL)
-        white = linv[...] * math.sqrt(n_cells)
         front = jnp.transpose(white) if it == ITERS - 1 else white
         high = front.astype(BF16)
         low = (front - high.astype(F32)).astype(BF16)
@@ -497,8 +491,8 @@
                 omega[:, pl.ds(i * blk, blk)] = ((flip[:rank] + flip[rank:]) * gene_scale).astype(BF16)
         else:
             for i in range(nx):
-                t = jnp.concatenate([wide_all[i, j] for j in range(nz)], axis=0)
-                load_out[pl.ds(i * blk, blk), :] = inner_contract(t, white, HIGHEST) * gene_scale
+                for j in range(nz):
+                    load_out[pl.ds(i * blk + j * zr, zr), :] = last[j * nx + i].astype(F32)
 
     leave.wait()
     for s in sent:
@@ -573,7 +567,7 @@
             V((nc, wide // nc, rank), BF16),
             V((nx, blk, rank), F32),
             V((nx, blk, rank), F32),
-            V((nx, nz, zr, rank), F32),
+            V((nc, zr, rank), BF16),
             V((nz, zr, rank), F32),
             V((nz, zr, rank), F32),
             V((2 * rank, rank), BF16),
@@ -596,8 +590,7 @@
             *pairs(nc),
             *pairs(nx),
             *pairs(nz),
-            *pairs(nz),
-            *pairs(nx),
+            *pairs(nc),
             *pairs(ITERS, ng),
             *pairs(ITERS, nx),
             *pairs(ITERS, nz),

time: 108 us -> 111 us (1.028)
  Pallas kernels: 106 us -> 108 us
    pallas_call x1, Pallas kernels: 103 us -> 105 us  [shards(): pl.pallas_call(functools.partial(kernel, dims), out_shape=(jax.ShapeDtype...]
where the time goes in v7:
time: 111 us; the launch traced here: 109 us
  Pallas kernels  108 us (97%)
    pallas_call x1, Pallas kernels, shards(): pl.pallas_call(functools.partial(kernel, dims), out_shape=(jax.ShapeDtype...  105 us
    pallas_call x1, Pallas kernels, shards(): pl.pallas_call(finish, grid=(BLOCKS,), out_shape=(jax.ShapeDtypeStruct((r...  3.19 us

profile of v7, /device:TPU:32, one launch (start us, length us, event | category | flops | bytes accessed | tf_op | source)
XLA Modules:
  0.0 108.8 jit_solution(7271105807990936665)
XLA Ops:
  0.6 105.0 %sweep.1 = (bf16[8,640,128]{2,1,0:T(8,128)(2,1)}, bf16[128,256]{1,0:T(8,128)(2,1)}, f32[512,128]{1,0:T(8,128)}) custom-call(s32[500,4864]{1,0:T(8,128)} %bitcast.2, bf16[500,128]{1,0:T(8,128)(2,1)} %sketch_hbm.1), custom_call_target="tpu_custom_call" | custom-call | tf_op jit(solution)/shard_map/sweep/pallas_call | solution.py:530
  105.6 3.2 %finish.1 = (f32[4864,128]{1,0:T(8,128)}, f32[500,128]{1,0:T(8,128)}) custom-call(bf16[5120,128]{1,0:T(8,128)(2,1)} %bitcast.3, bf16[128,256]{1,0:T(8,128)(2,1)} %get-tuple-element.6.white_ref, f32[512,128]{1,0:T(8,128)} %get-tuple-element.7.load_ref), custom_call_target="tpu_custom_call" | custom-call | tf_op jit(solution)/shard_map/finish/pallas_call | solution.py:605
